TPU v7x, 256 devices: a whole 4x4x8 slice. The times are simulated.
256 devices in a mesh: dp: 2 (over x_lo), fsdp: 16 (over x_hi, y, core), tensor: 8 (over z).
Axes of the slice: x: 4 (x_hi: 2, x_lo: 2; x = x_hi * 2 + x_lo), y: 4, z: 8, core: 2. Of those that a mesh axis runs over, the one named last changes fastest.
Arguments:
- hidden: bfloat16 [16384, 2048], P(('dp', 'fsdp'), 'tensor'), may hold values from -8 to 8
- norm_gain: bfloat16 [2048], P('tensor'), may hold values from 0.099609375 to 1.8984375
- head_weight: bfloat16 [2048, 32128], P('fsdp', 'tensor'), may hold values from -1 to 1
- token_ids: int32 [32, 512], P(('dp', 'fsdp')), may hold values from 0 to 32127
- lengths: int32 [32], P(('dp', 'fsdp')), may hold values from 128 to 512
- old_logp: float32 [32, 512], P(('dp', 'fsdp')), may hold values from -12.5 to -9.5
- advantages: float32 [32, 512], P(('dp', 'fsdp')), may hold values from -4 to 4
- rollout_logp: float32 [32, 512], P(('dp', 'fsdp'), 'tensor'), may hold values from -16 to -1
- rollout_row: int32 [32], P(('dp', 'fsdp')), may hold values from 0 to 31, each once
Outputs:
- new_logp: float32 [32, 512], P(('dp', 'fsdp'))
- token_loss: float32 [32, 512], P(('dp', 'fsdp'))
- summary: float32 [3], replicated
Inputs may be any that keep to these rules, and one draw needn't show every extreme that they name: `rollout_row`: every row 0 to 31 is named once.
All inputs are finite; a program needn't handle non-finite values.
Results may differ from a plain program's by a relative error of at most 0.0005.
The roundings to bfloat16 on the way count: a program that leaves them out, or rounds other values in their place, can miss the bound.
Values may be sent and summed in bfloat16 or wider, within the bound.
No kernel may reach another device: no remote copies, remote signals or barrier semaphores. Data moves between devices by JAX's collectives and lax.ppermute only.
A program may use at most 128 MiB of HBM per device.

v0:
```python
import jax
import jax.numpy as jnp
from jax import lax
from jax.sharding import PartitionSpec as P

clip_eps = 0.2
kl_coef = 0.2
log_limit = 10.0
norm_eps = 1e-06


def copy_for_each(array, axis):
    copies = jnp.broadcast_to(array, (lax.axis_size(axis), *array.shape))
    return lax.all_to_all(copies, axis, split_axis=0, concat_axis=0, tiled=True)


def taken_together(array, axis):
    everything = copy_for_each(array, axis)
    return jnp.max(everything, axis=0)


def taken_together_2(array, axis):
    everything = copy_for_each(array, axis)
    return jnp.sum(everything, axis=0)


def in_one(arrays, axis):
    line, at, outs = (jnp.concatenate([a.reshape(-1) for a in arrays]), 0, [])
    so_far = taken_together_2(line, axis)
    for a in arrays:
        outs.append(so_far[at : at + a.size].reshape(a.shape))
        at += a.size
    return tuple(outs)


def joined_along(tiles, dim):
    lengths = list(tiles.shape[1:])
    lengths[dim] *= tiles.shape[0]
    return jnp.moveaxis(tiles, 0, dim).reshape(lengths)


def collect(array, axis, dim):
    return joined_along(copy_for_each(array, axis), dim)


def token_terms(new_logp, old_logp, advantages, ref_logp, live_mask, prob_square):
    shift = new_logp - old_logp
    prob_ratio = jnp.exp(jnp.clip(shift, -log_limit, log_limit))
    clipped = jnp.clip(prob_ratio, 1.0 - clip_eps, 1.0 + clip_eps)
    plain_term = prob_ratio * advantages
    bounded_term = clipped * advantages
    surrogate = jnp.minimum(plain_term, bounded_term)
    ref_gap = ref_logp - new_logp
    gap_clip = jnp.clip(ref_gap, -log_limit, log_limit)
    kl_term = jnp.exp(gap_clip) - gap_clip - 1.0
    token_loss = live_mask * (kl_coef * kl_term - surrogate)
    inside_gap = (jnp.abs(ref_gap) < log_limit).astype(jnp.float32)
    inside_ratio = (jnp.abs(shift) < log_limit).astype(jnp.float32)
    active_term = (plain_term <= bounded_term).astype(jnp.float32)
    grad_coef = live_mask * (
        kl_coef * (1.0 - jnp.exp(gap_clip)) * inside_gap
        - advantages * prob_ratio * active_term * inside_ratio
    )
    grad_square = grad_coef * grad_coef * (prob_square - 2.0 * jnp.exp(new_logp) + 1.0)
    return (token_loss, live_mask * kl_term, grad_square)


def exp_sums(logits, row_max):
    shifted = jnp.exp(logits - row_max[:, None])
    return (jnp.sum(shifted, axis=1), jnp.sum(shifted * shifted, axis=1))


def vocab_stats(logits, flat_ids, col_start):
    col_ids = lax.broadcasted_iota(jnp.int32, logits.shape, 1) + col_start
    picked = jnp.sum(jnp.where(col_ids == flat_ids[:, None], logits, 0.0), axis=1)
    local_max = jnp.max(logits, axis=1)
    row_max = taken_together(local_max, "tensor")
    exp_sum, exp_square = exp_sums(logits, row_max)
    exp_sum, exp_square, picked = in_one((exp_sum, exp_square, picked), "tensor")
    return (row_max, exp_sum, exp_square, picked)


def shards(
    hidden,
    norm_gain,
    head_weight,
    token_ids,
    lengths,
    old_logp,
    advantages,
    rollout_logp,
    rollout_row,
):
    full_rows, full_gain = (collect(hidden, "tensor", 1), collect(norm_gain, "tensor", 0))
    values = full_rows.astype(jnp.float32)
    inv_rms = lax.rsqrt(jnp.mean(values * values, axis=1, keepdims=True) + norm_eps)
    normed = (values * inv_rms * full_gain.astype(jnp.float32)[None, :]).astype(jnp.bfloat16)
    flat_ids = token_ids.reshape(-1)
    vocab_cols = head_weight.shape[1]
    tensor_pos = lax.axis_index("tensor")
    logits = jnp.dot(
        normed,
        lax.all_gather(head_weight, "fsdp", axis=0, tiled=True),
        preferred_element_type=jnp.float32,
    )
    soft_stats = vocab_stats(logits, flat_ids, tensor_pos * vocab_cols)
    row_max, exp_sum, exp_square, picked = soft_stats
    new_logp = (picked - row_max - jnp.log(exp_sum)).reshape(token_ids.shape)
    prob_square = (exp_square / (exp_sum * exp_sum)).reshape(token_ids.shape)
    ref_all = collect(rollout_logp, ("dp", "fsdp"), 0)
    own_ref = jnp.take(ref_all, rollout_row, axis=0)
    ref_logp = collect(own_ref, "tensor", 1)
    positions = lax.broadcasted_iota(jnp.int32, token_ids.shape, 1)
    live_mask = (positions < lengths[:, None]).astype(jnp.float32)
    token_loss, kl_part, grad_part = token_terms(
        new_logp, old_logp, advantages, ref_logp, live_mask, prob_square
    )
    live_count, loss_sum, kl_sum, grad_sum = in_one(
        (jnp.sum(live_mask), jnp.sum(token_loss), jnp.sum(kl_part), jnp.sum(grad_part)),
        ("dp", "fsdp"),
    )
    summary = jnp.stack(
        [loss_sum / live_count, kl_sum / live_count, jnp.sqrt(grad_sum / live_count)]
    )
    return (new_logp, token_loss, summary)


def solution(mesh):
    in_specs = (
        P(("dp", "fsdp"), "tensor"),
        P("tensor"),
        P("fsdp", "tensor"),
        P(("dp", "fsdp"), None),
        P(("dp", "fsdp")),
        P(("dp", "fsdp"), None),
        P(("dp", "fsdp"), None),
        P(("dp", "fsdp"), "tensor"),
        P(("dp", "fsdp")),
    )
    out_specs = (P(("dp", "fsdp"), None), P(("dp", "fsdp"), None), P())
    return jax.shard_map(shards, mesh=mesh, in_specs=in_specs, out_specs=out_specs, check_vma=False)
```

profile of v0, /device:TPU:1, one launch (start us, length us, event | category | flops | bytes accessed | tf_op | source)
XLA Modules:
  0.0 218.8 jit_solution(17460148132570036709)
XLA Ops:
  7.2 0.7 all-gather.2.cloned.1.call-update
  7.9 0.7 broadcast_in_dim.42
  9.1 0.7 reduce.12
  9.8 0.6 reshape.211
  10.4 9.0 %all-to-all-start.1 = ((bf16[8,2,128]{2,1,0:T(2,128)(2,1)}), bf16[8,2,128]{2,1,0:T(2,128)(2,1)S(1)}, u32[]{:S(2)}, u32[]{:S(2)}) async-start(bf16[8,2,128]{2,1,0:T(2,128)(2,1)} %reshape.211), calls=%async_computation.1 | async-start | bytes 8192 | tf_op jit(solution)/shard_map/all_to_all | solution.py:14
  19.4 1.1 copy.14
  20.5 5.5 %all-to-all-done.1 = bf16[8,2,128]{2,1,0:T(2,128)(2,1)S(1)} async-done(((bf16[8,2,128]{2,1,0:T(2,128)(2,1)}), bf16[8,2,128]{2,1,0:T(2,128)(2,1)S(1)}, u32[]{:S(2)}, u32[]{:S(2)}) %all-to-all-start.1) | async-done | bytes 4128 | tf_op jit(solution)/shard_map/all_to_all | solution.py:14
  25.9 1.5 broadcast_in_dim.41
  27.4 3.6 %all-to-all-start = ((bf16[8,512,256]{1,2,0:T(8,128)(2,1)}), bf16[8,512,256]{1,2,0:T(8,128)(2,1)S(1)}, u32[]{:S(2)}, u32[]{:S(2)}) async-start(bf16[8,512,256]{1,2,0:T(8,128)(2,1)} %broadcast_in_dim.41), calls=%async_computation | async-start | bytes 4194304 | tf_op jit(solution)/shard_map/all_to_all | solution.py:14
  31.8 50.9 %all-to-all-done = bf16[8,512,256]{1,2,0:T(8,128)(2,1)S(1)} async-done(((bf16[8,512,256]{1,2,0:T(8,128)(2,1)}), bf16[8,512,256]{1,2,0:T(8,128)(2,1)S(1)}, u32[]{:S(2)}, u32[]{:S(2)}) %all-to-all-start) | async-done | bytes 2097184 | tf_op jit(solution)/shard_map/all_to_all | solution.py:14
  82.6 0.6 broadcast_in_dim.48
  83.2 7.6 %all-to-all-start.4 = ((f32[32,1,64]{2,1,0:T(1,128)}), f32[32,1,64]{2,1,0:T(1,128)S(1)}, u32[]{:S(2)}, u32[]{:S(2)}) async-start(f32[32,1,64]{2,1,0:T(1,128)} %broadcast_in_dim.48), calls=%async_computation.4 | async-start | bytes 32768 | tf_op jit(solution)/shard_map/all_to_all | solution.py:14
  91.4 2.0 fusion.2
  93.4 43.2 %all-gather.2.cloned.1.call-done = bf16[2048,4016]{0,1:T(8,128)(2,1)} async-done(((bf16[128,4016]{0,1:T(8,128)(2,1)}), bf16[2048,4016]{0,1:T(8,128)(2,1)}) %all-gather.2.cloned.1.call-update) | async-done | bytes 16449552 | tf_op jit(solution)/shard_map/all_gather | solution.py:103
  136.5 14.8 %fusion.18 = (f32[512]{0:T(512)S(1)}, f32[512,4016]{0,1:T(8,128)}) fusion(bf16[2048,4016]{0,1:T(8,128)(2,1)} %all-gather.2.cloned.1.call-done, bf16[512,2048]{0,1:T(8,128)(2,1)} %fusion.2), kind=kOutput, calls=%fused_computation.43 | convolution fusion | flops 8424218112 | bytes 26773504 | tf_op jit(solution)/shard_map/dot_general | solution.py:101
  151.3 0.6 broadcast_in_dim.43
  151.9 6.7 %all-to-all-start.2 = ((f32[8,1,512]{2,1,0:T(1,128)}), f32[8,1,512]{2,1,0:T(1,128)S(1)}, u32[]{:S(2)}, u32[]{:S(2)}) async-start(f32[8,1,512]{2,1,0:T(1,128)} %broadcast_in_dim.43), calls=%async_computation.2 | async-start | bytes 32768 | tf_op jit(solution)/shard_map/all_to_all | solution.py:14
  158.7 6.6 %all-to-all-done.2 = f32[8,1,512]{2,1,0:T(1,128)S(1)} async-done(((f32[8,1,512]{2,1,0:T(1,128)}), f32[8,1,512]{2,1,0:T(1,128)S(1)}, u32[]{:S(2)}, u32[]{:S(2)}) %all-to-all-start.2) | async-done | bytes 16416 | tf_op jit(solution)/shard_map/all_to_all | solution.py:14
  165.3 0.6 broadcast_in_dim.50
  165.9 3.3 %all-to-all-start.5 = ((f32[8,1,64]{2,1,0:T(1,128)}), f32[8,1,64]{2,1,0:T(1,128)S(1)}, u32[]{:S(2)}, u32[]{:S(2)}) async-start(f32[8,1,64]{2,1,0:T(1,128)} %broadcast_in_dim.50), calls=%async_computation.5 | async-start | bytes 8192 | tf_op jit(solution)/shard_map/all_to_all | solution.py:14
  169.3 5.4 %fusion = (f32[512]{0:T(512)S(1)}, f32[512]{0:T(512)S(1)}, f32[512]{0:T(512)S(1)}) fusion(f32[512,4016]{0,1:T(8,128)} %get-tuple-element.29, f32[512]{0:T(512)S(1)} %reduce_max.19, s32[512]{0:T(512)S(1)} %bitcast.36, s32[4016]{0:T(1024)S(1)} %iota_add_fusion), kind=kLoop, calls=%fused_computation.3 | loop fusion | flops 14391808 | bytes 8251072 | tf_op jit(solution)/shard_map/reduce_sum | solution.py:70
  174.7 1.0 all-to-all-done.5
  175.7 0.6 broadcast_in_dim.45
  176.3 5.6 %all-to-all-start.3 = ((f32[8,1,1536]{2,1,0:T(1,128)}), f32[8,1,1536]{2,1,0:T(1,128)S(1)}, u32[]{:S(2)}, u32[]{:S(2)}) async-start(f32[8,1,1536]{2,1,0:T(1,128)} %broadcast_in_dim.45), calls=%async_computation.3 | async-start | bytes 98304 | tf_op jit(solution)/shard_map/all_to_all | solution.py:14
  183.1 0.7 reduce.11
  183.9 5.1 %all-to-all-done.3 = f32[8,1,1536]{2,1,0:T(1,128)S(1)} async-done(((f32[8,1,1536]{2,1,0:T(1,128)}), f32[8,1,1536]{2,1,0:T(1,128)S(1)}, u32[]{:S(2)}, u32[]{:S(2)}) %all-to-all-start.3) | async-done | bytes 49184 | tf_op jit(solution)/shard_map/all_to_all | solution.py:14
  189.2 0.6 reduce_sum.97
  189.8 1.3 fusion.15
  191.1 2.6 %pad_maximum_fusion.1 = f32[4]{0:T(128)S(1)} fusion(f32[1]{0:T(128)} %bitcast.17, f32[1]{0:T(128)} %bitcast.14, f32[1]{0:T(128)} %bitcast.12, f32[1]{0:T(128)} %bitcast.11), kind=kLoop, calls=%fused_computation.38 | loop fusion | flops 12 | bytes 32 | tf_op jit(solution)/shard_map/concatenate | solution.py:28
  193.7 13.1 %all_to_all.39 = f32[32,1,4]{2,1,0:T(1,128)S(1)} all-to-all(f32[32,1,4]{2,1,0:T(1,128)S(1)} %broadcast_in_dim.51), channel_id=1, replica_groups=mesh['dp'=2,'fsdp'=16,'tensor'=8] {'dp','fsdp'}, dimensions={0} | all-to-all | bytes 1024 | tf_op jit(solution)/shard_map/all_to_all | solution.py:14
  206.9 0.7 fusion.17
  211.3 0.6 pad_maximum_fusion.2
  (30 shorter events, 2.0 us)
Async XLA Ops:
  7.2 75.5 %copy-start.4 = (f32[1,64]{1,0:T(1,128)S(1)}, f32[1,64]{1,0:T(1,128)}, u32[]{:S(2)}) copy-start(f32[1,64]{1,0:T(1,128)} %param.16) | copy-start | bytes 772
  7.2 129.3 %all-gather.2.cloned.1.call-start = ((), (), s32[]{:S(2)}) async-start(), calls=%async_computation.7 | async-start | bytes 17477632 | tf_op jit(solution)/shard_map/all_gather | solution.py:103
  10.4 15.6 %all-to-all-start.1 = ((bf16[8,2,128]{2,1,0:T(2,128)(2,1)}), bf16[8,2,128]{2,1,0:T(2,128)(2,1)S(1)}, u32[]{:S(2)}, u32[]{:S(2)}) async-start(bf16[8,2,128]{2,1,0:T(2,128)(2,1)} %reshape.211), calls=%async_computation.1 | async-start | bytes 8192 | tf_op jit(solution)/shard_map/all_to_all | solution.py:14
  27.4 55.2 %all-to-all-start = ((bf16[8,512,256]{1,2,0:T(8,128)(2,1)}), bf16[8,512,256]{1,2,0:T(8,128)(2,1)S(1)}, u32[]{:S(2)}, u32[]{:S(2)}) async-start(bf16[8,512,256]{1,2,0:T(8,128)(2,1)} %broadcast_in_dim.41), calls=%async_computation | async-start | bytes 4194304 | tf_op jit(solution)/shard_map/all_to_all | solution.py:14
  83.2 68.1 %all-to-all-start.4 = ((f32[32,1,64]{2,1,0:T(1,128)}), f32[32,1,64]{2,1,0:T(1,128)S(1)}, u32[]{:S(2)}, u32[]{:S(2)}) async-start(f32[32,1,64]{2,1,0:T(1,128)} %broadcast_in_dim.48), calls=%async_computation.4 | async-start | bytes 32768 | tf_op jit(solution)/shard_map/all_to_all | solution.py:14
  93.4 75.9 %copy-start.3 = (s32[1,512]{1,0:T(1,128)S(1)}, s32[1,512]{1,0:T(1,128)}, u32[]{:S(2)}) copy-start(s32[1,512]{1,0:T(1,128)} %param.12) | copy-start | bytes 6148
  151.9 13.4 %all-to-all-start.2 = ((f32[8,1,512]{2,1,0:T(1,128)}), f32[8,1,512]{2,1,0:T(1,128)S(1)}, u32[]{:S(2)}, u32[]{:S(2)}) async-start(f32[8,1,512]{2,1,0:T(1,128)} %broadcast_in_dim.43), calls=%async_computation.2 | async-start | bytes 32768 | tf_op jit(solution)/shard_map/all_to_all | solution.py:14
  165.9 9.8 %all-to-all-start.5 = ((f32[8,1,64]{2,1,0:T(1,128)}), f32[8,1,64]{2,1,0:T(1,128)S(1)}, u32[]{:S(2)}, u32[]{:S(2)}) async-start(f32[8,1,64]{2,1,0:T(1,128)} %broadcast_in_dim.50), calls=%async_computation.5 | async-start | bytes 8192 | tf_op jit(solution)/shard_map/all_to_all | solution.py:14
  169.3 20.6 %copy-start.1 = (f32[1,512]{1,0:T(1,128)S(1)}, f32[1,512]{1,0:T(1,128)}, u32[]{:S(2)}) copy-start(f32[1,512]{1,0:T(1,128)} %param.15) | copy-start | bytes 6148
  169.3 20.6 %copy-start.2 = (f32[1,512]{1,0:T(1,128)S(1)}, f32[1,512]{1,0:T(1,128)}, u32[]{:S(2)}) copy-start(f32[1,512]{1,0:T(1,128)} %param.14) | copy-start | bytes 6148
  176.3 12.7 %all-to-all-start.3 = ((f32[8,1,1536]{2,1,0:T(1,128)}), f32[8,1,1536]{2,1,0:T(1,128)S(1)}, u32[]{:S(2)}, u32[]{:S(2)}) async-start(f32[8,1,1536]{2,1,0:T(1,128)} %broadcast_in_dim.45), calls=%async_computation.3 | async-start | bytes 98304 | tf_op jit(solution)/shard_map/all_to_all | solution.py:14
  189.1 22.9 %copy-start = (f32[512]{0:T(512)}, f32[512]{0:T(512)S(1)}, u32[]{:S(2)}) copy-start(f32[512]{0:T(512)S(1)} %get-tuple-element.20) | copy-start | bytes 6148
Sparse Core Ops, SparseCore 0:
  10.5 125.9 all-gather.1
where the time goes:
time: 219 us
  waiting for transfers between devices  113 us (52%)
  starting transfers between devices  36 us (16%)
  between operations  19.3 us (9%)
  matrix products  14.8 us (7%)
  other arithmetic  14.5 us (7%)
  blocking collectives  13.1 us (6%)
  local copies, waits for them, and re-layouts  8.21 us (4%)
    all_to_all x6, waiting for transfers between devices, copy_for_each(): return lax.all_to_all(copies, axis, split_axis=0, concat_axis=0, tiled=True)  69 us
    all_gather x1, waiting for transfers between devices, shards(): lax.all_gather(head_weight, 'fsdp', axis=0, tiled=True)  43.2 us
    all_to_all x6, starting transfers between devices, copy_for_each(): return lax.all_to_all(copies, axis, split_axis=0, concat_axis=0, tiled=True)  35.9 us
    dot_general x1, matrix products, shards(): jnp.dot(normed, lax.all_gather(head_weight, 'fsdp', axis=0, tiled=True),...  14.8 us
    all_to_all x1, blocking collectives, copy_for_each(): return lax.all_to_all(copies, axis, split_axis=0, concat_axis=0, tiled=True)  13.1 us
    reduce_sum x1, other arithmetic, exp_sums(): return (jnp.sum(shifted, axis=1), jnp.sum(shifted * shifted, axis=1))  5.43 us
    broadcast_in_dim x8, local copies, waits for them, and re-layouts, copy_for_each(): copies = jnp.broadcast_to(array, (lax.axis_size(axis), *array.shape))  5.14 us
  transfers between devices with their start and end apart: 7, of which 6 were waited for; matrix products, arithmetic and copies ran while one was open for 14% of the time, Pallas kernels for 0%

commit v1 on v0

v1 whole, which is shorter than its diff:
```python
import jax
import jax.numpy as jnp
from jax import lax
from jax.experimental import pallas as pl
from jax.experimental.pallas import tpu as pltpu
from jax.sharding import Mesh, PartitionSpec as P


clip_eps = 0.2
kl_coef = 0.2
log_limit = 10.0
norm_eps = 1e-06

HALF = 2008
ROWS = 128
FEAT = 256
TOK = 512
PART = TOK + 16
TILE = 256


def shift(n, k):
    return [(i, (i + k) % n) for i in range(n)]


def x_position(x):
    return (x % 2) * 2 + x // 2


X_NEAR = [(x_position(a), x_position(b)) for a, b in ((1, 2), (2, 1), (3, 0), (0, 3))]


def prepare_kernel(hidden_ref, gain_ref, ids_ref, head_ref, stream_ref, mine_ref, other_ref, sem):
    dp = lax.axis_index("dp")
    at = pl.multiple_of(dp * HALF, 8)
    away = pl.multiple_of((1 - dp) * HALF, 8)
    copies = [
        pltpu.make_async_copy(head_ref.at[pl.ds(away, HALF)], other_ref, sem),
        pltpu.make_async_copy(head_ref.at[pl.ds(at, HALF)], mine_ref, sem),
    ]
    for c in copies:
        c.start()
    stream_ref[:TOK, :] = hidden_ref[...]
    ids = ids_ref[...]
    digits = [(ids // 256).astype(jnp.float32), (ids % 256).astype(jnp.float32)]
    rows = [gain_ref[...].astype(jnp.float32).reshape(1, FEAT)] + [d[:, h * FEAT : (h + 1) * FEAT] for d in digits for h in range(2)]
    rows.append(jnp.zeros((PART - TOK - 5, FEAT), jnp.float32))
    stream_ref[TOK:, :] = jnp.concatenate(rows, axis=0).astype(jnp.bfloat16)
    for c in copies:
        c.wait()


def prepare(hidden, gain, ids, slices):
    vmem = pl.BlockSpec(memory_space=pltpu.VMEM)
    any_spec = pl.BlockSpec(memory_space=pl.ANY)
    half = jax.ShapeDtypeStruct((HALF, ROWS), jnp.bfloat16)
    return pl.pallas_call(
        prepare_kernel,
        out_shape=(jax.ShapeDtypeStruct((PART, FEAT), jnp.bfloat16), half, half),
        in_specs=[vmem] * 3 + [any_spec],
        out_specs=[vmem] * 3,
        scratch_shapes=[pltpu.SemaphoreType.DMA],
        name="prepare",
    )(hidden, gain, ids, slices)


def head_kernel(*refs):
    tok_sets = [refs[0:8], refs[8:16]]
    heads = refs[16:26]
    ref_ref, out_ref, w_buf, t_buf, *lhs, even, odd, sem_t, sem_p, sem_w = refs[26:]
    dp, xh, y, core, tensor = [lax.axis_index(a) for a in ("dp", "xh", "y", "core", "tensor")]

    def copy(src, dst, sem):
        c = pltpu.make_async_copy(src, dst, sem)
        c.start()
        return c

    sems = (sem_t, sem_p)

    def fetch_tokens(s):
        return [copy(tok_sets[s][k], t_buf.at[s, k], sems[s]) for k in range(8)]

    lanes_of = [pl.ds(i * ROWS, ROWS) for i in range(16)]
    t_copies = [fetch_tokens(0)]
    w_copies = []
    for s in range(2):
        own, near, near_passed, far, far_passed = heads[5 * s : 5 * s + 5]
        at = 8 * s
        for h in range(2):
            w_copies.append(copy(own.at[h], w_buf.at[:, lanes_of[at + h]], sem_w))
            w_copies.append(copy(near.at[h], w_buf.at[:, lanes_of[at + 2 + h]], sem_w))
            w_copies.append(copy(near_passed.at[h], w_buf.at[:, lanes_of[at + 5 - h]], sem_w))
            last = pltpu.make_async_copy(far.at[h], w_buf.at[:, lanes_of[at + 6 + h]], sem_w)
            passed_last = pltpu.make_async_copy(far_passed.at[h], w_buf.at[:, lanes_of[at + 7 - h]], sem_w)

            @pl.when(core == s)
            def _():
                last.start()

            @pl.when(core != s)
            def _():
                passed_last.start()

            w_copies.append(last)
    t_copies.append(fetch_tokens(1))

    way = 2 * core - 1

    def place(k):
        if k == 0:
            offset = 0
        elif k == 7:
            offset = 4
        else:
            step = (k + 1) // 2
            offset = -step if k % 2 == 1 else step
        z = lax.rem(tensor + offset + 8, 8)
        zh, zy = lax.div(z, 4), lax.rem(z, 4)
        step = lax.rem(way * (zy - y) + 4, 4)
        order = jnp.where(step == 0, 0, jnp.where(step == 1, 1, jnp.where(step == 3, 2, 3)))
        return jnp.where(zh == xh, 0, 4) + order

    places = [place(k) * FEAT for k in range(8)]

    def norm(n):
        s, half = divmod(n, 2)
        for i in range(TILE // 32):
            at = slice(half * TILE + i * 32, half * TILE + i * 32 + 32)
            to = slice(i * 32, i * 32 + 32)
            total = None
            for k in range(8):
                v = t_buf[s, k, at, :].astype(jnp.float32)
                v = v * v
                v = v[:, :128] + v[:, 128:]
                total = v if total is None else total + v
            mean = jnp.sum(total, axis=1, keepdims=True) * (1.0 / 2048)
            scale = jnp.broadcast_to(lax.rsqrt(mean + norm_eps), (32, 128))
            for k in range(8):
                v = t_buf[s, k, at, :].astype(jnp.float32)
                gain = t_buf[s, k, TOK : TOK + 1, :].astype(jnp.float32)
                for h in range(2):
                    cut = slice(h * 128, h * 128 + 128)
                    part = (v[:, cut] * scale * gain[:, cut]).astype(jnp.bfloat16)
                    lhs[n][to, pl.ds(pl.multiple_of(places[k] + (core ^ h) * 128, 128), 128)] = part

    for c in t_copies[0]:
        c.wait()
    norm(0)
    for c in t_copies[1]:
        c.wait()
    for c in w_copies:
        c.wait()

    base, away = 8 * dp, 8 - 8 * dp
    start = tensor * (2 * HALF) + dp * HALF

    def matmul(n, buf):
        buf[...] = lax.dot_general(
            w_buf[...],
            lhs[n][...],
            (((1,), (1,)), ((), ())),
            preferred_element_type=jnp.float32,
        )

    cuts = [slice(i, min(i + 64, HALF)) for i in range(0, HALF, 64)]

    def fold(x, op):
        parts = [x[i : i + 8] for i in range(0, x.shape[0], 8)]
        while len(parts) > 1:
            pairs = [op(a, b) for a, b in zip(parts[::2], parts[1::2])]
            parts = pairs + parts[len(parts) // 2 * 2 :]
        return parts[0]

    row = lax.broadcasted_iota(jnp.int32, (64, 128), 0)

    def take(n, buf):
        s, half = divmod(n, 2)
        block = base if s == 0 else away
        for lt in range(TILE // 128):
            lanes = slice(lt * 128, lt * 128 + 128)
            digits = [t_buf[s, 0, TOK + 1 + r : TOK + 2 + r, lanes].astype(jnp.float32) for r in (half, 2 + half)]
            ids = (digits[0] * 256.0 + digits[1]).astype(jnp.int32) - start
            top = None
            for cut in cuts:
                part = fold(buf[cut, lanes], jnp.maximum)
                top = part if top is None else jnp.maximum(top, part)
            top = jnp.max(top, axis=0, keepdims=True)
            total = square = pick = jnp.zeros((8, 128), jnp.float32)
            for cut in cuts:
                x = buf[cut, lanes]
                e = jnp.exp(x - top)
                total = total + fold(e, jnp.add)
                square = square + fold(e * e, jnp.add)
                hit = row[: x.shape[0]] == ids - cut.start
                pick = pick + fold(jnp.where(hit, x, 0.0), jnp.add)
            line = half * 2 + lt
            out_ref[block, line : line + 1, :] = top
            for r, v in ((4, total), (8, square), (12, pick)):
                out_ref[block, r + line : r + line + 1, :] = jnp.sum(v, axis=0, keepdims=True)

    steps = 2 * TOK // TILE
    bufs = (even, odd)
    for n in range(steps):
        matmul(n, bufs[n % 2])
        if n + 1 < steps:
            norm(n + 1)
        if n > 0:
            take(n - 1, bufs[(n - 1) % 2])
    take(steps - 1, bufs[(steps - 1) % 2])
    out_ref[base, 16:24, :] = ref_ref[...]
    out_ref[away, 16:24, :] = ref_ref[...]
    for j in range(1, 8):
        out_ref[base + j] = out_ref[base]
        out_ref[away + j] = out_ref[away]


def head_stats(own_toks, partner_toks, heads, ref):
    any_spec = pl.BlockSpec(memory_space=pl.ANY)
    vmem = pl.BlockSpec(memory_space=pltpu.VMEM)
    return pl.pallas_call(
        head_kernel,
        out_shape=jax.ShapeDtypeStruct((16, 24, 128), jnp.float32),
        in_specs=[any_spec] * 26 + [vmem],
        out_specs=vmem,
        scratch_shapes=[
            pltpu.VMEM((HALF, 2048), jnp.bfloat16),
            pltpu.VMEM((2, 8, PART, FEAT), jnp.bfloat16),
            *[pltpu.VMEM((TILE, 2048), jnp.bfloat16) for _ in range(2 * TOK // TILE)],
            pltpu.VMEM((HALF, TILE), jnp.float32),
            pltpu.VMEM((HALF, TILE), jnp.float32),
            pltpu.SemaphoreType.DMA,
            pltpu.SemaphoreType.DMA,
            pltpu.SemaphoreType.DMA,
        ],
        compiler_params=pltpu.CompilerParams(vmem_limit_bytes=56 * 1024 * 1024),
        cost_estimate=pl.CostEstimate(
            flops=4 * TOK * HALF * 2048, bytes_accessed=13 * 2**20, transcendentals=2 * TOK * HALF
        ),
        name="head_stats",
    )(*own_toks, *partner_toks, *heads, ref)


def combine_kernel(length_ref, got_ref, old_ref, adv_ref, logp_ref, loss_ref, parts_ref):
    dp, length = lax.axis_index("dp"), length_ref[0]
    tops = got_ref[:, 0:4, :]
    row_max = jnp.max(tops, axis=0)
    scale = jnp.exp(tops - row_max[None])
    exp_sum = jnp.sum(got_ref[:, 4:8, :] * scale, axis=0)
    exp_square = jnp.sum(got_ref[:, 8:12, :] * (scale * scale), axis=0)
    picked = jnp.sum(got_ref[:, 12:16, :], axis=0)
    new_logp = picked - row_max - jnp.log(exp_sum)
    prob_square = exp_square / (exp_sum * exp_sum)

    def rows(ref):
        return jnp.concatenate([ref[:, i * 128 : (i + 1) * 128] for i in range(4)], axis=0)

    ref_rows = [got_ref[8 * dp + i, 16:17, :64] for i in range(8)]
    ref_logp = jnp.concatenate(
        [jnp.concatenate(ref_rows[2 * i : 2 * i + 2], axis=1) for i in range(4)], axis=0
    )
    positions = lax.broadcasted_iota(jnp.int32, (4, 128), 0) * 128
    positions = positions + lax.broadcasted_iota(jnp.int32, (4, 128), 1)
    live_mask = (positions < length).astype(jnp.float32)
    token_loss, kl_part, grad_part = token_terms(
        new_logp, rows(old_ref), rows(adv_ref), ref_logp, live_mask, prob_square
    )
    for i in range(4):
        logp_ref[:, i * 128 : (i + 1) * 128] = new_logp[i : i + 1, :]
        loss_ref[:, i * 128 : (i + 1) * 128] = token_loss[i : i + 1, :]
    lane = lax.broadcasted_iota(jnp.int32, (1, 128), 1)
    line = jnp.zeros((1, 128), jnp.float32)
    for i, term in enumerate((live_mask, token_loss, kl_part, grad_part)):
        total = jnp.sum(jnp.sum(term, axis=0, keepdims=True), axis=1, keepdims=True)
        line = jnp.where(lane == i, total, line)
    parts_ref[...] = jnp.broadcast_to(line[None], (32, 1, 128))


def combine(lengths, got, old_logp, advantages):
    vmem = pl.BlockSpec(memory_space=pltpu.VMEM)
    line = jax.ShapeDtypeStruct((1, TOK), jnp.float32)
    return pl.pallas_call(
        combine_kernel,
        out_shape=(line, line, jax.ShapeDtypeStruct((32, 1, 128), jnp.float32)),
        in_specs=[pl.BlockSpec(memory_space=pltpu.SMEM)] + [vmem] * 3,
        out_specs=[vmem] * 3,
        name="combine",
    )(lengths, got, old_logp, advantages)


def token_terms(new_logp, old_logp, advantages, ref_logp, live_mask, prob_square):
    diff = new_logp - old_logp
    prob_ratio = jnp.exp(jnp.clip(diff, -log_limit, log_limit))
    clipped = jnp.clip(prob_ratio, 1.0 - clip_eps, 1.0 + clip_eps)
    plain_term = prob_ratio * advantages
    bounded_term = clipped * advantages
    surrogate = jnp.minimum(plain_term, bounded_term)
    ref_gap = ref_logp - new_logp
    gap_clip = jnp.clip(ref_gap, -log_limit, log_limit)
    kl_term = jnp.exp(gap_clip) - gap_clip - 1.0
    token_loss = live_mask * (kl_coef * kl_term - surrogate)
    inside_gap = (jnp.abs(ref_gap) < log_limit).astype(jnp.float32)
    inside_ratio = (jnp.abs(diff) < log_limit).astype(jnp.float32)
    active_term = (plain_term <= bounded_term).astype(jnp.float32)
    grad_coef = live_mask * (
        kl_coef * (1.0 - jnp.exp(gap_clip)) * inside_gap
        - advantages * prob_ratio * active_term * inside_ratio
    )
    grad_square = grad_coef * grad_coef * (prob_square - 2.0 * jnp.exp(new_logp) + 1.0)
    return (token_loss, live_mask * kl_term, grad_square)


def two_way_y():
    up = [(2 * i, 2 * ((i + 1) % 4)) for i in range(4)]
    down = [(2 * i + 1, 2 * ((i - 1) % 4) + 1) for i in range(4)]
    return up + down


def token_ring(own, far_step):
    back, ahead = own, own
    out = [own]
    for _ in range(1, 4):
        back = lax.ppermute(back, "tensor", shift(8, 1))
        ahead = lax.ppermute(ahead, "tensor", shift(8, -1))
        out += [back, ahead]
    far = back if far_step > 0 else ahead
    return out + [lax.ppermute(far, "tensor", shift(8, far_step))]


def head_ring(block, far_core):
    near = lax.ppermute(block, ("y", "core"), two_way_y())
    pairs = [p for p in two_way_y() if p[0] % 2 == far_core]
    far = lax.ppermute(near, ("y", "core"), pairs)
    near_passed = lax.ppermute(near, "core", shift(2, 1))
    far_passed = lax.ppermute(far, "core", [(far_core, 1 - far_core)])
    return [block, near, near_passed, far, far_passed]


def steps(hidden, norm_gain, head_weight, token_ids, lengths, old_logp, advantages, rollout_logp, rollout_row):
    slices = head_weight.T
    stream, mine, other = prepare(hidden, norm_gain, token_ids, slices)
    partner = lax.ppermute(stream, "dp", shift(2, 1))
    own_toks = token_ring(stream, 1)

    near = lax.ppermute(other, ("dp", "xh"), X_NEAR)
    heads = head_ring(jnp.stack([mine, lax.ppermute(mine, "core", shift(2, 1))]), 0)
    heads += head_ring(jnp.stack([near, lax.ppermute(near, "core", shift(2, 1))]), 1)
    partner_toks = token_ring(partner, -1)

    refs = jnp.broadcast_to(rollout_logp, (32, 1, 64))
    refs = lax.all_to_all(refs, ("dp", "xh", "y", "core"), 0, 0, tiled=True)
    own_ref = lax.dynamic_index_in_dim(refs[:, 0], rollout_row[0], 0)
    own_ref = jnp.pad(own_ref, ((0, 7), (0, 64)))

    send = head_stats(own_toks, partner_toks, heads, own_ref)
    got = lax.all_to_all(send, ("dp", "tensor"), 0, 0, tiled=True)
    new_logp, token_loss, parts = combine(lengths, got, old_logp, advantages)
    totals = jnp.sum(lax.all_to_all(parts, ("dp", "xh", "y", "core"), 0, 0, tiled=True), axis=(0, 1))
    ratio = totals[1:4] / totals[0]
    summary = jnp.where(lax.iota(jnp.int32, 3) == 2, jnp.sqrt(ratio), ratio)
    return (new_logp, token_loss, summary)


def solution(mesh):
    fine = Mesh(mesh.devices.reshape(2, 2, 4, 2, 8), ("dp", "xh", "y", "core", "tensor"))
    rows = ("dp", "xh", "y", "core")
    in_specs = (
        P(rows, "tensor"),
        P("tensor"),
        P(("xh", "y", "core"), "tensor"),
        P(rows, None),
        P(rows),
        P(rows, None),
        P(rows, None),
        P(rows, "tensor"),
        P(rows),
    )
    out_specs = (P(rows, None), P(rows, None), P())
    return jax.shard_map(steps, mesh=fine, in_specs=in_specs, out_specs=out_specs, check_vma=False)
```

time: 219 us -> 181 us (0.83)
  waiting for transfers between devices: 113 us -> 85.1 us
  Pallas kernels: 0 us -> 24.1 us
  between operations: 19.3 us -> 2.15 us
  starting transfers between devices: 36 us -> 51.8 us
  matrix products: 14.8 us -> 0 us
  other arithmetic: 14.5 us -> 1.91 us
  local copies, waits for them, and re-layouts: 8.21 us -> 2.48 us
    ppermute x0 -> x26, waiting for transfers between devices: none -> 72.2 us  [the longest x6 22.8 us: token_ring(): ahead = lax.ppermute(ahead, 'tensor', shift(8, -1))]
    all_to_all x6 -> x2, waiting for transfers between devices: 69 us -> 12.9 us  [the longest x1 6.78 us: steps(): got = lax.all_to_all(send, ('dp', 'tensor'), 0, 0, tiled=True)]
    all_gather x1 -> x0, waiting for transfers between devices: 43.2 us -> none  [shards(): lax.all_gather(head_weight, 'fsdp', axis=0, tiled=True)]
    ppermute x0 -> x26, starting transfers between devices: none -> 41.5 us  [the longest x6 13 us: token_ring(): ahead = lax.ppermute(ahead, 'tensor', shift(8, -1))]
    all_to_all x6 -> x2, starting transfers between devices: 35.9 us -> 10.3 us  [the longest x1 6.74 us: steps(): refs = lax.all_to_all(refs, ('dp', 'xh', 'y', 'core'), 0, 0, tiled=True)]
    pallas_call x0 -> x3, Pallas kernels: none -> 24.1 us  [the longest x1 19.1 us: head_stats(): pl.pallas_call(head_kernel, out_shape=jax.ShapeDtypeStruct((16, 24, 128),...]
    dot_general x1 -> x0, matrix products: 14.8 us -> none  [shards(): jnp.dot(normed, lax.all_gather(head_weight, 'fsdp', axis=0, tiled=True),...]
    reduce_sum x6 -> x1, other arithmetic: 7.95 us -> 0.05 us  [steps(): jnp.sum(lax.all_to_all(parts, ('dp', 'xh', 'y', 'core'), 0, 0, tiled=True...]
  transfers between devices with their start and end apart: 7 -> 28, of which waited for: 6 -> 14; matrix products, arithmetic and copies ran while one was open for 14% -> 1% of each run, Pallas kernels for 0% -> 0%
where the time goes in v1:
time: 181 us; the launch traced here: 180 us
  waiting for transfers between devices  85.1 us (47%)
  starting transfers between devices  51.8 us (29%)
  Pallas kernels  24.1 us (13%)
  blocking collectives  12.8 us (7%)
  local copies, waits for them, and re-layouts  2.48 us (1%)
  between operations  2.15 us (1%)
  other arithmetic  1.91 us (1%)
    ppermute x6, waiting for transfers between devices, token_ring(): ahead = lax.ppermute(ahead, 'tensor', shift(8, -1))  22.8 us
    pallas_call x1, Pallas kernels, head_stats(): pl.pallas_call(head_kernel, out_shape=jax.ShapeDtypeStruct((16, 24, 128),...  19.1 us
    ppermute x2, waiting for transfers between devices, head_ring(): near = lax.ppermute(block, ('y', 'core'), two_way_y())  18.3 us
    ppermute x6, starting transfers between devices, token_ring(): ahead = lax.ppermute(ahead, 'tensor', shift(8, -1))  13 us
    all_to_all x1, blocking collectives, steps(): lax.all_to_all(parts, ('dp', 'xh', 'y', 'core'), 0, 0, tiled=True)  12.8 us
    ppermute x6, waiting for transfers between devices, token_ring(): back = lax.ppermute(back, 'tensor', shift(8, 1))  11.7 us
    ppermute x1, waiting for transfers between devices, steps(): near = lax.ppermute(other, ('dp', 'xh'), X_NEAR)  9.75 us
    ppermute x2, waiting for transfers between devices, token_ring(): return out + [lax.ppermute(far, 'tensor', shift(8, far_step))]  9.69 us
  transfers between devices with their start and end apart: 28, of which 14 were waited for; matrix products, arithmetic and copies ran while one was open for 1% of the time, Pallas kernels for 0%

profile of v1, /device:TPU:1, one launch (start us, length us, event | category | flops | bytes accessed | tf_op | source)
XLA Modules:
  0.0 180.3 jit_solution(17671412078423458857)
XLA Ops:
  0.6 3.3 %prepare.1 = (bf16[528,256]{1,0:T(8,128)(2,1)}, bf16[2008,128]{1,0:T(8,128)(2,1)}, bf16[2008,128]{1,0:T(8,128)(2,1)}) custom-call(bf16[512,256]{1,0:T(8,128)(2,1)} %hidden_ref.1, bf16[256]{0:T(256)(128)(2,1)} %gain_ref.1, s32[1,512]{1,0:T(1,128)} %ids_ref.1, bf16[4016,128]{1,0:T(8,128)(2,1)} %bitcast.14), custom_call_target="tpu_custom_call" | custom-call | tf_op jit(solution)/shard_map/prepare/pallas_call | solution.py:57
  3.9 3.4 %collective-permute-start.20 = (bf16[2008,128]{1,0:T(8,128)(2,1)}, bf16[2008,128]{1,0:T(8,128)(2,1)S(1)}, u32[]{:S(2)}, u32[]{:S(2)}) collective-permute-start(bf16[2008,128]{1,0:T(8,128)(2,1)} %get-tuple-element.11), channel_id=1, source_target_pairs={{128,64},{64,128},{192,0},{0,192},{129,65},{65,129},{193,1},{1,193... | collective-permute-start | bytes 1542152 | tf_op jit(solution)/shard_map/ppermute | solution.py:344
  8.2 9.7 %collective-permute-done.20 = bf16[2008,128]{1,0:T(8,128)(2,1)S(1)} collective-permute-done((bf16[2008,128]{1,0:T(8,128)(2,1)}, bf16[2008,128]{1,0:T(8,128)(2,1)S(1)}, u32[]{:S(2)}, u32[]{:S(2)}) %collective-permute-start.20) | collective-permute-done | bytes 514080 | tf_op jit(solution)/shard_map/ppermute | solution.py:344
  18.0 2.2 %collective-permute-start.21 = (bf16[2008,128]{1,0:T(8,128)(2,1)S(1)}, bf16[2008,128]{1,0:T(8,128)(2,1)S(1)}, u32[]{:S(2)}, u32[]{:S(2)}) collective-permute-start(bf16[2008,128]{1,0:T(8,128)(2,1)S(1)} %collective-permute-done.20), channel_id=1, source_target_pairs={{0,8},{8,0},{1,9},{9,1},{2,10},{10,2},{3,11},{11,3},{4,12},{12,4},... | collective-permute-start | bytes 1542152 | tf_op jit(solution)/shard_map/ppermute | solution.py:346
  21.3 3.0 %collective-permute-start.16 = (bf16[2,2008,128]{2,1,0:T(8,128)(2,1)S(1)}, bf16[2,2008,128]{2,1,0:T(8,128)(2,1)S(1)}, u32[]{:S(2)}, u32[]{:S(2)}) collective-permute-start(bf16[2,2008,128]{2,1,0:T(8,128)(2,1)S(1)} %pad_maximum_fusion.refs_16_), channel_id=1, source_target_pairs={{0,16},{16,32},{32,48},{48,0},{8,56},{24,8},{40,24},{56,40},{1,17}... | collective-permute-start | bytes 3084296 | tf_op jit(solution)/shard_map/ppermute | solution.py:330
  25.3 1.7 collective-permute-start
  26.9 8.9 %collective-permute-done.16.refs_17_ = bf16[2,2008,128]{2,1,0:T(8,128)(2,1)S(1)} collective-permute-done((bf16[2,2008,128]{2,1,0:T(8,128)(2,1)S(1)}, bf16[2,2008,128]{2,1,0:T(8,128)(2,1)S(1)}, u32[]{:S(2)}, u32[]{:S(2)}) %collective-permute-start.16) | collective-permute-done | bytes 1028128 | tf_op jit(solution)/shard_map/ppermute | solution.py:330
  35.8 1.6 collective-permute-start.18
  37.5 9.4 %collective-permute-done.22.refs_22_ = bf16[2,2008,128]{2,1,0:T(8,128)(2,1)S(1)} collective-permute-done((bf16[2,2008,128]{2,1,0:T(8,128)(2,1)S(1)}, bf16[2,2008,128]{2,1,0:T(8,128)(2,1)S(1)}, u32[]{:S(2)}, u32[]{:S(2)}) %collective-permute-start.22) | collective-permute-done | bytes 1028128 | tf_op jit(solution)/shard_map/ppermute | solution.py:330
  46.9 5.0 %collective-permute-start.24 = (bf16[2,2008,128]{2,1,0:T(8,128)(2,1)S(1)}, bf16[2,2008,128]{2,1,0:T(8,128)(2,1)}, u32[]{:S(2)}, u32[]{:S(2)}) collective-permute-start(bf16[2,2008,128]{2,1,0:T(8,128)(2,1)S(1)} %collective-permute-done.22.refs_22_), channel_id=1, source_target_pairs={{8,56},{24,8},{40,24},{56,40},{9,57},{25,9},{41,25},{57,41},{10,58... | collective-permute-start | bytes 3084296 | tf_op jit(solution)/shard_map/ppermute | solution.py:332
  51.9 5.7 %collective-permute-start.1 = (bf16[528,256]{1,0:T(8,128)(2,1)S(1)}, bf16[528,256]{1,0:T(8,128)(2,1)S(1)}, u32[]{:S(2)}, u32[]{:S(2)}) collective-permute-start(bf16[528,256]{1,0:T(8,128)(2,1)S(1)} %copy-done.6), channel_id=1, source_target_pairs={{0,7},{1,0},{2,1},{3,2},{4,3},{5,4},{6,5},{7,6},{8,15},{9,8},{10,9... | collective-permute-start | bytes 811016 | tf_op jit(solution)/shard_map/ppermute | solution.py:323
  59.0 4.8 %collective-permute-done.1.refs_2_ = bf16[528,256]{1,0:T(8,128)(2,1)S(1)} collective-permute-done((bf16[528,256]{1,0:T(8,128)(2,1)S(1)}, bf16[528,256]{1,0:T(8,128)(2,1)S(1)}, u32[]{:S(2)}, u32[]{:S(2)}) %collective-permute-start.1) | collective-permute-done | bytes 270368 | tf_op jit(solution)/shard_map/ppermute | solution.py:323
  63.8 4.3 %collective-permute-done.9.refs_10_ = bf16[528,256]{1,0:T(8,128)(2,1)S(1)} collective-permute-done((bf16[528,256]{1,0:T(8,128)(2,1)S(1)}, bf16[528,256]{1,0:T(8,128)(2,1)S(1)}, u32[]{:S(2)}, u32[]{:S(2)}) %collective-permute-start.9) | collective-permute-done | bytes 270368 | tf_op jit(solution)/shard_map/ppermute | solution.py:323
  68.2 3.1 %collective-permute-start.3 = (bf16[528,256]{1,0:T(8,128)(2,1)S(1)}, bf16[528,256]{1,0:T(8,128)(2,1)S(1)}, u32[]{:S(2)}, u32[]{:S(2)}) collective-permute-start(bf16[528,256]{1,0:T(8,128)(2,1)S(1)} %collective-permute-done.1.refs_2_), channel_id=1, source_target_pairs={{0,7},{1,0},{2,1},{3,2},{4,3},{5,4},{6,5},{7,6},{8,15},{9,8},{10,9... | collective-permute-start | bytes 811016 | tf_op jit(solution)/shard_map/ppermute | solution.py:323
  71.4 1.2 collective-permute-done.2.refs_3_
  72.8 4.8 %collective-permute-done.3.refs_4_ = bf16[528,256]{1,0:T(8,128)(2,1)S(1)} collective-permute-done((bf16[528,256]{1,0:T(8,128)(2,1)S(1)}, bf16[528,256]{1,0:T(8,128)(2,1)S(1)}, u32[]{:S(2)}, u32[]{:S(2)}) %collective-permute-start.3) | collective-permute-done | bytes 270368 | tf_op jit(solution)/shard_map/ppermute | solution.py:323
  77.6 5.5 %collective-permute-done.11.refs_12_ = bf16[528,256]{1,0:T(8,128)(2,1)S(1)} collective-permute-done((bf16[528,256]{1,0:T(8,128)(2,1)S(1)}, bf16[528,256]{1,0:T(8,128)(2,1)S(1)}, u32[]{:S(2)}, u32[]{:S(2)}) %collective-permute-start.11) | collective-permute-done | bytes 270368 | tf_op jit(solution)/shard_map/ppermute | solution.py:323
  83.1 3.1 %collective-permute-start.5 = (bf16[528,256]{1,0:T(8,128)(2,1)S(1)}, bf16[528,256]{1,0:T(8,128)(2,1)S(1)}, u32[]{:S(2)}, u32[]{:S(2)}) collective-permute-start(bf16[528,256]{1,0:T(8,128)(2,1)S(1)} %collective-permute-done.3.refs_4_), channel_id=1, source_target_pairs={{0,7},{1,0},{2,1},{3,2},{4,3},{5,4},{6,5},{7,6},{8,15},{9,8},{10,9... | collective-permute-start | bytes 811016 | tf_op jit(solution)/shard_map/ppermute | solution.py:323
  86.4 1.4 collective-permute-done.4.refs_5_
  88.3 3.4 %collective-permute-done.5.refs_6_ = bf16[528,256]{1,0:T(8,128)(2,1)S(1)} collective-permute-done((bf16[528,256]{1,0:T(8,128)(2,1)S(1)}, bf16[528,256]{1,0:T(8,128)(2,1)S(1)}, u32[]{:S(2)}, u32[]{:S(2)}) %collective-permute-start.5) | collective-permute-done | bytes 270368 | tf_op jit(solution)/shard_map/ppermute | solution.py:323
  91.6 2.0 %collective-permute-start.23 = (bf16[2,2008,128]{2,1,0:T(8,128)(2,1)S(1)}, bf16[2,2008,128]{2,1,0:T(8,128)(2,1)}, u32[]{:S(2)}, u32[]{:S(2)}) collective-permute-start(bf16[2,2008,128]{2,1,0:T(8,128)(2,1)S(1)} %collective-permute-done.22.refs_22_), channel_id=1, source_target_pairs={{0,8},{8,0},{1,9},{9,1},{2,10},{10,2},{3,11},{11,3},{4,12},{12,4},... | collective-permute-start | bytes 3084296 | tf_op jit(solution)/shard_map/ppermute | solution.py:333
  93.7 1.3 collective-permute-start.19
  95.0 5.0 %collective-permute-start.25 = (bf16[2,2008,128]{2,1,0:T(8,128)(2,1)}, bf16[2,2008,128]{2,1,0:T(8,128)(2,1)}, u32[]{:S(2)}, u32[]{:S(2)}) collective-permute-start(bf16[2,2008,128]{2,1,0:T(8,128)(2,1)} %collective-permute-done.24.refs_24_), channel_id=1, source_target_pairs={{8,0},{9,1},{10,2},{11,3},{12,4},{13,5},{14,6},{15,7},{24,16},{25,... | collective-permute-start | bytes 3084296 | tf_op jit(solution)/shard_map/ppermute | solution.py:334
  100.1 9.0 %collective-permute-done.12.refs_13_ = bf16[528,256]{1,0:T(8,128)(2,1)S(1)} collective-permute-done((bf16[528,256]{1,0:T(8,128)(2,1)S(1)}, bf16[528,256]{1,0:T(8,128)(2,1)S(1)}, u32[]{:S(2)}, u32[]{:S(2)}) %collective-permute-start.12) | collective-permute-done | bytes 270368 | tf_op jit(solution)/shard_map/ppermute | solution.py:322
  109.1 9.7 %collective-permute-done.6.refs_7_ = bf16[528,256]{1,0:T(8,128)(2,1)S(1)} collective-permute-done((bf16[528,256]{1,0:T(8,128)(2,1)S(1)}, bf16[528,256]{1,0:T(8,128)(2,1)S(1)}, u32[]{:S(2)}, u32[]{:S(2)}) %collective-permute-start.6) | collective-permute-done | bytes 270368 | tf_op jit(solution)/shard_map/ppermute | solution.py:326
  120.2 6.7 %all-to-all-start = ((f32[32,1,64]{2,1,0:T(1,128)}), f32[32,1,64]{2,1,0:T(1,128)S(1)}, u32[]{:S(2)}, u32[]{:S(2)}) async-start(f32[32,1,64]{2,1,0:T(1,128)} %broadcast_in_dim.3), calls=%async_computation | async-start | bytes 32768 | tf_op jit(solution)/shard_map/all_to_all | solution.py:350
  127.6 6.1 %all-to-all-done = f32[32,1,64]{2,1,0:T(1,128)S(1)} async-done(((f32[32,1,64]{2,1,0:T(1,128)}), f32[32,1,64]{2,1,0:T(1,128)S(1)}, u32[]{:S(2)}, u32[]{:S(2)}) %all-to-all-start) | async-done | bytes 8224 | tf_op jit(solution)/shard_map/all_to_all | solution.py:350
  134.4 19.1 %head_stats.1 = f32[16,24,128]{2,1,0:T(8,128)} custom-call(bf16[528,256]{1,0:T(8,128)(2,1)} %get-tuple-element.9.refs_0_, bf16[528,256]{1,0:T(8,128)(2,1)} %copy-done.8, bf16[528,256]{1,0:T(8,128)(2,1)} %copy-done.9, bf16[528,256]{1,0:T(8,128)(2,1)} %copy-done.12, bf16[528,256]{1,0:T(8,128)(2,1)} %copy-done.13, bf16[528,256]{1,0:T(8,128)(2,1)} %copy-done.16, ...), custom_call_target="tpu_custom_call" | custom-call | flops 8422162432 | bytes 13631488 | tf_op jit(solution)/shard_map/head_stats/pallas_call | solution.py:220
  153.4 3.5 %all-to-all-start.1 = ((f32[16,24,128]{2,1,0:T(8,128)}), f32[16,24,128]{2,1,0:T(8,128)S(1)}, u32[]{:S(2)}, u32[]{:S(2)}) async-start(f32[16,24,128]{2,1,0:T(8,128)} %head_stats.1), calls=%async_computation.1 | async-start | bytes 393216 | tf_op jit(solution)/shard_map/all_to_all | solution.py:355
  157.6 6.8 %all-to-all-done.1.got_ref = f32[16,24,128]{2,1,0:T(8,128)S(1)} async-done(((f32[16,24,128]{2,1,0:T(8,128)}), f32[16,24,128]{2,1,0:T(8,128)S(1)}, u32[]{:S(2)}, u32[]{:S(2)}) %all-to-all-start.1) | async-done | bytes 196640 | tf_op jit(solution)/shard_map/all_to_all | solution.py:355
  165.1 1.7 combine.1
  166.8 12.8 %all_to_all.15 = f32[32,1,128]{2,1,0:T(1,128)S(1)} all-to-all(f32[32,1,128]{2,1,0:T(1,128)} %get-tuple-element.14), channel_id=1, replica_groups=mesh['dp'=2,'xh'=2,'y'=4,'core'=2,'tensor'=8] {'dp','xh','y','core'}, dimensions={0} | all-to-all | bytes 32768 | tf_op jit(solution)/shard_map/all_to_all | solution.py:357
  (75 shorter events, 8.9 us)
Async XLA Ops:
  3.9 14.1 %collective-permute-start.20 = (bf16[2008,128]{1,0:T(8,128)(2,1)}, bf16[2008,128]{1,0:T(8,128)(2,1)S(1)}, u32[]{:S(2)}, u32[]{:S(2)}) collective-permute-start(bf16[2008,128]{1,0:T(8,128)(2,1)} %get-tuple-element.11), channel_id=1, source_target_pairs={{128,64},{64,128},{192,0},{0,192},{129,65},{65,129},{193,1},{1,193... | collective-permute-start | bytes 1542152 | tf_op jit(solution)/shard_map/ppermute | solution.py:344
  7.3 12.9 %collective-permute-start.15 = (bf16[2008,128]{1,0:T(8,128)(2,1)}, bf16[2008,128]{1,0:T(8,128)(2,1)S(1)}, u32[]{:S(2)}, u32[]{:S(2)}) collective-permute-start(bf16[2008,128]{1,0:T(8,128)(2,1)} %get-tuple-element.10), channel_id=1, source_target_pairs={{0,8},{8,0},{1,9},{9,1},{2,10},{10,2},{3,11},{11,3},{4,12},{12,4},... | collective-permute-start | bytes 1542152 | tf_op jit(solution)/shard_map/ppermute | solution.py:345
  18.0 6.3 %collective-permute-start.21 = (bf16[2008,128]{1,0:T(8,128)(2,1)S(1)}, bf16[2008,128]{1,0:T(8,128)(2,1)S(1)}, u32[]{:S(2)}, u32[]{:S(2)}) collective-permute-start(bf16[2008,128]{1,0:T(8,128)(2,1)S(1)} %collective-permute-done.20), channel_id=1, source_target_pairs={{0,8},{8,0},{1,9},{9,1},{2,10},{10,2},{3,11},{11,3},{4,12},{12,4},... | collective-permute-start | bytes 1542152 | tf_op jit(solution)/shard_map/ppermute | solution.py:346
  21.3 14.5 %collective-permute-start.16 = (bf16[2,2008,128]{2,1,0:T(8,128)(2,1)S(1)}, bf16[2,2008,128]{2,1,0:T(8,128)(2,1)S(1)}, u32[]{:S(2)}, u32[]{:S(2)}) collective-permute-start(bf16[2,2008,128]{2,1,0:T(8,128)(2,1)S(1)} %pad_maximum_fusion.refs_16_), channel_id=1, source_target_pairs={{0,16},{16,32},{32,48},{48,0},{8,56},{24,8},{40,24},{56,40},{1,17}... | collective-permute-start | bytes 3084296 | tf_op jit(solution)/shard_map/ppermute | solution.py:330
  24.4 109.9 %copy-start.1 = (bf16[2,2008,128]{2,1,0:T(8,128)(2,1)}, bf16[2,2008,128]{2,1,0:T(8,128)(2,1)S(1)}, u32[]{:S(2)}) copy-start(bf16[2,2008,128]{2,1,0:T(8,128)(2,1)S(1)} %pad_maximum_fusion.1.refs_21_) | copy-start | bytes 3084292
  24.4 22.4 %collective-permute-start.22 = (bf16[2,2008,128]{2,1,0:T(8,128)(2,1)S(1)}, bf16[2,2008,128]{2,1,0:T(8,128)(2,1)S(1)}, u32[]{:S(2)}, u32[]{:S(2)}) collective-permute-start(bf16[2,2008,128]{2,1,0:T(8,128)(2,1)S(1)} %pad_maximum_fusion.1.refs_21_), channel_id=1, source_target_pairs={{0,16},{16,32},{32,48},{48,0},{8,56},{24,8},{40,24},{56,40},{1,17}... | collective-permute-start | bytes 3084296 | tf_op jit(solution)/shard_map/ppermute | solution.py:330
  25.3 94.3 %copy-start.3 = (f32[1,64]{1,0:T(1,128)S(1)}, f32[1,64]{1,0:T(1,128)}, u32[]{:S(2)}) copy-start(f32[1,64]{1,0:T(1,128)} %param.16) | copy-start | bytes 772
  25.3 32.3 %collective-permute-start.7 = (bf16[528,256]{1,0:T(8,128)(2,1)S(1)}, bf16[528,256]{1,0:T(8,128)(2,1)S(1)}, u32[]{:S(2)}, u32[]{:S(2)}) collective-permute-start(bf16[528,256]{1,0:T(8,128)(2,1)S(1)} %copy-done.6), channel_id=1, source_target_pairs={{0,128},{128,0},{1,129},{129,1},{2,130},{130,2},{3,131},{131,3},{4... | collective-permute-start | bytes 811016 | tf_op jit(solution)/shard_map/ppermute | solution.py:341
  25.3 33.0 %collective-permute-start = (bf16[528,256]{1,0:T(8,128)(2,1)S(1)}, bf16[528,256]{1,0:T(8,128)(2,1)S(1)}, u32[]{:S(2)}, u32[]{:S(2)}) collective-permute-start(bf16[528,256]{1,0:T(8,128)(2,1)S(1)} %copy-done.6), channel_id=1, source_target_pairs={{0,1},{1,2},{2,3},{3,4},{4,5},{5,6},{6,7},{7,0},{8,9},{9,10},{10,1... | collective-permute-start | bytes 811016 | tf_op jit(solution)/shard_map/ppermute | solution.py:322
  35.8 98.5 %copy-start.4 = (bf16[2,2008,128]{2,1,0:T(8,128)(2,1)}, bf16[2,2008,128]{2,1,0:T(8,128)(2,1)S(1)}, u32[]{:S(2)}) copy-start(bf16[2,2008,128]{2,1,0:T(8,128)(2,1)S(1)} %collective-permute-done.16.refs_17_) | copy-start | bytes 3084292
  35.8 57.9 %collective-permute-start.18 = (bf16[2,2008,128]{2,1,0:T(8,128)(2,1)S(1)}, bf16[2,2008,128]{2,1,0:T(8,128)(2,1)}, u32[]{:S(2)}, u32[]{:S(2)}) collective-permute-start(bf16[2,2008,128]{2,1,0:T(8,128)(2,1)S(1)} %collective-permute-done.16.refs_17_), channel_id=1, source_target_pairs={{0,16},{16,32},{32,48},{48,0},{1,17},{17,33},{33,49},{49,1},{2,18}... | collective-permute-start | bytes 3084296 | tf_op jit(solution)/shard_map/ppermute | solution.py:332
  46.9 87.5 %copy-start.5 = (bf16[2,2008,128]{2,1,0:T(8,128)(2,1)}, bf16[2,2008,128]{2,1,0:T(8,128)(2,1)S(1)}, u32[]{:S(2)}) copy-start(bf16[2,2008,128]{2,1,0:T(8,128)(2,1)S(1)} %collective-permute-done.22.refs_22_) | copy-start | bytes 3084292
  46.9 48.1 %collective-permute-start.24 = (bf16[2,2008,128]{2,1,0:T(8,128)(2,1)S(1)}, bf16[2,2008,128]{2,1,0:T(8,128)(2,1)}, u32[]{:S(2)}, u32[]{:S(2)}) collective-permute-start(bf16[2,2008,128]{2,1,0:T(8,128)(2,1)S(1)} %collective-permute-done.22.refs_22_), channel_id=1, source_target_pairs={{8,56},{24,8},{40,24},{56,40},{9,57},{25,9},{41,25},{57,41},{10,58... | collective-permute-start | bytes 3084296 | tf_op jit(solution)/shard_map/ppermute | solution.py:332
  51.9 12.0 %collective-permute-start.1 = (bf16[528,256]{1,0:T(8,128)(2,1)S(1)}, bf16[528,256]{1,0:T(8,128)(2,1)S(1)}, u32[]{:S(2)}, u32[]{:S(2)}) collective-permute-start(bf16[528,256]{1,0:T(8,128)(2,1)S(1)} %copy-done.6), channel_id=1, source_target_pairs={{0,7},{1,0},{2,1},{3,2},{4,3},{5,4},{6,5},{7,6},{8,15},{9,8},{10,9... | collective-permute-start | bytes 811016 | tf_op jit(solution)/shard_map/ppermute | solution.py:323
  57.5 10.6 %collective-permute-start.9 = (bf16[528,256]{1,0:T(8,128)(2,1)S(1)}, bf16[528,256]{1,0:T(8,128)(2,1)S(1)}, u32[]{:S(2)}, u32[]{:S(2)}) collective-permute-start(bf16[528,256]{1,0:T(8,128)(2,1)S(1)} %collective-permute-done.7.refs_8_), channel_id=1, source_target_pairs={{0,7},{1,0},{2,1},{3,2},{4,3},{5,4},{6,5},{7,6},{8,15},{9,8},{10,9... | collective-permute-start | bytes 811016 | tf_op jit(solution)/shard_map/ppermute | solution.py:323
  58.3 13.0 %collective-permute-start.8 = (bf16[528,256]{1,0:T(8,128)(2,1)S(1)}, bf16[528,256]{1,0:T(8,128)(2,1)S(1)}, u32[]{:S(2)}, u32[]{:S(2)}) collective-permute-start(bf16[528,256]{1,0:T(8,128)(2,1)S(1)} %collective-permute-done.7.refs_8_), channel_id=1, source_target_pairs={{0,1},{1,2},{2,3},{3,4},{4,5},{5,6},{6,7},{7,0},{8,9},{9,10},{10,1... | collective-permute-start | bytes 811016 | tf_op jit(solution)/shard_map/ppermute | solution.py:322
  63.8 8.7 %collective-permute-start.2 = (bf16[528,256]{1,0:T(8,128)(2,1)S(1)}, bf16[528,256]{1,0:T(8,128)(2,1)S(1)}, u32[]{:S(2)}, u32[]{:S(2)}) collective-permute-start(bf16[528,256]{1,0:T(8,128)(2,1)S(1)} %collective-permute-done.refs_1_), channel_id=1, source_target_pairs={{0,1},{1,2},{2,3},{3,4},{4,5},{5,6},{6,7},{7,0},{8,9},{9,10},{10,1... | collective-permute-start | bytes 811016 | tf_op jit(solution)/shard_map/ppermute | solution.py:322
  68.2 9.4 %collective-permute-start.3 = (bf16[528,256]{1,0:T(8,128)(2,1)S(1)}, bf16[528,256]{1,0:T(8,128)(2,1)S(1)}, u32[]{:S(2)}, u32[]{:S(2)}) collective-permute-start(bf16[528,256]{1,0:T(8,128)(2,1)S(1)} %collective-permute-done.1.refs_2_), channel_id=1, source_target_pairs={{0,7},{1,0},{2,1},{3,2},{4,3},{5,4},{6,5},{7,6},{8,15},{9,8},{10,9... | collective-permute-start | bytes 811016 | tf_op jit(solution)/shard_map/ppermute | solution.py:323
  71.3 11.8 %collective-permute-start.11 = (bf16[528,256]{1,0:T(8,128)(2,1)S(1)}, bf16[528,256]{1,0:T(8,128)(2,1)S(1)}, u32[]{:S(2)}, u32[]{:S(2)}) collective-permute-start(bf16[528,256]{1,0:T(8,128)(2,1)S(1)} %collective-permute-done.9.refs_10_), channel_id=1, source_target_pairs={{0,7},{1,0},{2,1},{3,2},{4,3},{5,4},{6,5},{7,6},{8,15},{9,8},{10,9... | collective-permute-start | bytes 811016 | tf_op jit(solution)/shard_map/ppermute | solution.py:323
  72.6 13.6 %collective-permute-start.10 = (bf16[528,256]{1,0:T(8,128)(2,1)S(1)}, bf16[528,256]{1,0:T(8,128)(2,1)S(1)}, u32[]{:S(2)}, u32[]{:S(2)}) collective-permute-start(bf16[528,256]{1,0:T(8,128)(2,1)S(1)} %collective-permute-done.8.refs_9_), channel_id=1, source_target_pairs={{0,1},{1,2},{2,3},{3,4},{4,5},{5,6},{6,7},{7,0},{8,9},{9,10},{10,1... | collective-permute-start | bytes 811016 | tf_op jit(solution)/shard_map/ppermute | solution.py:322
  77.6 10.3 %collective-permute-start.4 = (bf16[528,256]{1,0:T(8,128)(2,1)S(1)}, bf16[528,256]{1,0:T(8,128)(2,1)S(1)}, u32[]{:S(2)}, u32[]{:S(2)}) collective-permute-start(bf16[528,256]{1,0:T(8,128)(2,1)S(1)} %collective-permute-done.2.refs_3_), channel_id=1, source_target_pairs={{0,1},{1,2},{2,3},{3,4},{4,5},{5,6},{6,7},{7,0},{8,9},{9,10},{10,1... | collective-permute-start | bytes 811016 | tf_op jit(solution)/shard_map/ppermute | solution.py:322
  83.1 8.6 %collective-permute-start.5 = (bf16[528,256]{1,0:T(8,128)(2,1)S(1)}, bf16[528,256]{1,0:T(8,128)(2,1)S(1)}, u32[]{:S(2)}, u32[]{:S(2)}) collective-permute-start(bf16[528,256]{1,0:T(8,128)(2,1)S(1)} %collective-permute-done.3.refs_4_), channel_id=1, source_target_pairs={{0,7},{1,0},{2,1},{3,2},{4,3},{5,4},{6,5},{7,6},{8,15},{9,8},{10,9... | collective-permute-start | bytes 811016 | tf_op jit(solution)/shard_map/ppermute | solution.py:323
  86.2 13.8 %collective-permute-start.13 = (bf16[528,256]{1,0:T(8,128)(2,1)S(1)}, bf16[528,256]{1,0:T(8,128)(2,1)}, u32[]{:S(2)}, u32[]{:S(2)}) collective-permute-start(bf16[528,256]{1,0:T(8,128)(2,1)S(1)} %collective-permute-done.11.refs_12_), channel_id=1, source_target_pairs={{0,7},{1,0},{2,1},{3,2},{4,3},{5,4},{6,5},{7,6},{8,15},{9,8},{10,9... | collective-permute-start | bytes 811016 | tf_op jit(solution)/shard_map/ppermute | solution.py:323
  87.9 46.4 %collective-permute-start.17 = (bf16[2,2008,128]{2,1,0:T(8,128)(2,1)S(1)}, bf16[2,2008,128]{2,1,0:T(8,128)(2,1)}, u32[]{:S(2)}, u32[]{:S(2)}) collective-permute-start(bf16[2,2008,128]{2,1,0:T(8,128)(2,1)S(1)} %collective-permute-done.16.refs_17_), channel_id=1, source_target_pairs={{0,8},{8,0},{1,9},{9,1},{2,10},{10,2},{3,11},{11,3},{4,12},{12,4},... | collective-permute-start | bytes 3084296 | tf_op jit(solution)/shard_map/ppermute | solution.py:333
  91.6 42.6 %collective-permute-start.23 = (bf16[2,2008,128]{2,1,0:T(8,128)(2,1)S(1)}, bf16[2,2008,128]{2,1,0:T(8,128)(2,1)}, u32[]{:S(2)}, u32[]{:S(2)}) collective-permute-start(bf16[2,2008,128]{2,1,0:T(8,128)(2,1)S(1)} %collective-permute-done.22.refs_22_), channel_id=1, source_target_pairs={{0,8},{8,0},{1,9},{9,1},{2,10},{10,2},{3,11},{11,3},{4,12},{12,4},... | collective-permute-start | bytes 3084296 | tf_op jit(solution)/shard_map/ppermute | solution.py:333
  93.7 40.6 %collective-permute-start.19 = (bf16[2,2008,128]{2,1,0:T(8,128)(2,1)}, bf16[2,2008,128]{2,1,0:T(8,128)(2,1)}, u32[]{:S(2)}, u32[]{:S(2)}) collective-permute-start(bf16[2,2008,128]{2,1,0:T(8,128)(2,1)} %collective-permute-done.18.refs_19_), channel_id=1, source_target_pairs={{0,8},{1,9},{2,10},{3,11},{4,12},{5,13},{6,14},{7,15},{16,24},{17,... | collective-permute-start | bytes 3084296 | tf_op jit(solution)/shard_map/ppermute | solution.py:334
  95.0 39.3 %collective-permute-start.25 = (bf16[2,2008,128]{2,1,0:T(8,128)(2,1)}, bf16[2,2008,128]{2,1,0:T(8,128)(2,1)}, u32[]{:S(2)}, u32[]{:S(2)}) collective-permute-start(bf16[2,2008,128]{2,1,0:T(8,128)(2,1)} %collective-permute-done.24.refs_24_), channel_id=1, source_target_pairs={{8,0},{9,1},{10,2},{11,3},{12,4},{13,5},{14,6},{15,7},{24,16},{25,... | collective-permute-start | bytes 3084296 | tf_op jit(solution)/shard_map/ppermute | solution.py:334
  100.0 9.1 %collective-permute-start.12 = (bf16[528,256]{1,0:T(8,128)(2,1)S(1)}, bf16[528,256]{1,0:T(8,128)(2,1)S(1)}, u32[]{:S(2)}, u32[]{:S(2)}) collective-permute-start(bf16[528,256]{1,0:T(8,128)(2,1)S(1)} %collective-permute-done.10.refs_11_), channel_id=1, source_target_pairs={{0,1},{1,2},{2,3},{3,4},{4,5},{5,6},{6,7},{7,0},{8,9},{9,10},{10,1... | collective-permute-start | bytes 811016 | tf_op jit(solution)/shard_map/ppermute | solution.py:322
  109.1 9.7 %collective-permute-start.6 = (bf16[528,256]{1,0:T(8,128)(2,1)S(1)}, bf16[528,256]{1,0:T(8,128)(2,1)S(1)}, u32[]{:S(2)}, u32[]{:S(2)}) collective-permute-start(bf16[528,256]{1,0:T(8,128)(2,1)S(1)} %collective-permute-done.4.refs_5_), channel_id=1, source_target_pairs={{0,1},{1,2},{2,3},{3,4},{4,5},{5,6},{6,7},{7,0},{8,9},{9,10},{10,1... | collective-permute-start | bytes 811016 | tf_op jit(solution)/shard_map/ppermute | solution.py:326
  118.8 15.5 %collective-permute-start.14 = (bf16[528,256]{1,0:T(8,128)(2,1)}, bf16[528,256]{1,0:T(8,128)(2,1)}, u32[]{:S(2)}, u32[]{:S(2)}) collective-permute-start(bf16[528,256]{1,0:T(8,128)(2,1)} %collective-permute-done.13.refs_14_), channel_id=1, source_target_pairs={{0,7},{1,0},{2,1},{3,2},{4,3},{5,4},{6,5},{7,6},{8,15},{9,8},{10,9... | collective-permute-start | bytes 811016 | tf_op jit(solution)/shard_map/ppermute | solution.py:326
  120.2 13.5 %all-to-all-start = ((f32[32,1,64]{2,1,0:T(1,128)}), f32[32,1,64]{2,1,0:T(1,128)S(1)}, u32[]{:S(2)}, u32[]{:S(2)}) async-start(f32[32,1,64]{2,1,0:T(1,128)} %broadcast_in_dim.3), calls=%async_computation | async-start | bytes 32768 | tf_op jit(solution)/shard_map/all_to_all | solution.py:350
  153.4 11.0 %all-to-all-start.1 = ((f32[16,24,128]{2,1,0:T(8,128)}), f32[16,24,128]{2,1,0:T(8,128)S(1)}, u32[]{:S(2)}, u32[]{:S(2)}) async-start(f32[16,24,128]{2,1,0:T(8,128)} %head_stats.1), calls=%async_computation.1 | async-start | bytes 393216 | tf_op jit(solution)/shard_map/all_to_all | solution.py:355
  (16 other events, 421.2 us)

commit v2 on v1

--- a/solution.py
+++ b/solution.py
@@ -30,7 +30,9 @@
 X_NEAR = [(x_position(a), x_position(b)) for a, b in ((1, 2), (2, 1), (3, 0), (0, 3))]
 
 
-def prepare_kernel(hidden_ref, gain_ref, ids_ref, head_ref, stream_ref, mine_ref, other_ref, sem):
+def prepare_kernel(
+    hidden_ref, gain_ref, ids_ref, logp_ref, head_ref, stream_ref, mine_ref, other_ref, rows_ref, sem
+):
     dp = lax.axis_index("dp")
     at = pl.multiple_of(dp * HALF, 8)
     away = pl.multiple_of((1 - dp) * HALF, 8)
@@ -40,6 +42,7 @@
     ]
     for c in copies:
         c.start()
+    rows_ref[...] = jnp.broadcast_to(logp_ref[...][None], rows_ref.shape)
     stream_ref[:TOK, :] = hidden_ref[...]
     ids = ids_ref[...]
     digits = [(ids // 256).astype(jnp.float32), (ids % 256).astype(jnp.float32)]
@@ -50,18 +53,23 @@
         c.wait()
 
 
-def prepare(hidden, gain, ids, slices):
+def prepare(hidden, gain, ids, logp, slices):
     vmem = pl.BlockSpec(memory_space=pltpu.VMEM)
     any_spec = pl.BlockSpec(memory_space=pl.ANY)
     half = jax.ShapeDtypeStruct((HALF, ROWS), jnp.bfloat16)
     return pl.pallas_call(
         prepare_kernel,
-        out_shape=(jax.ShapeDtypeStruct((PART, FEAT), jnp.bfloat16), half, half),
-        in_specs=[vmem] * 3 + [any_spec],
-        out_specs=[vmem] * 3,
+        out_shape=(
+            jax.ShapeDtypeStruct((PART, FEAT), jnp.bfloat16),
+            half,
+            half,
+            jax.ShapeDtypeStruct((32, 1, 64), jnp.float32),
+        ),
+        in_specs=[vmem] * 4 + [any_spec],
+        out_specs=[vmem] * 4,
         scratch_shapes=[pltpu.SemaphoreType.DMA],
         name="prepare",
-    )(hidden, gain, ids, slices)
+    )(hidden, gain, ids, logp, slices)
 
 
 def head_kernel(*refs):
@@ -207,8 +215,9 @@
         if n > 0:
             take(n - 1, bufs[(n - 1) % 2])
     take(steps - 1, bufs[(steps - 1) % 2])
-    out_ref[base, 16:24, :] = ref_ref[...]
-    out_ref[away, 16:24, :] = ref_ref[...]
+    for block in (base, away):
+        out_ref[block, 16:24, :] = jnp.zeros((8, 128), jnp.float32)
+        out_ref[block, 16:17, :64] = ref_ref[...]
     for j in range(1, 8):
         out_ref[base + j] = out_ref[base]
         out_ref[away + j] = out_ref[away]
@@ -337,7 +346,7 @@
 
 def steps(hidden, norm_gain, head_weight, token_ids, lengths, old_logp, advantages, rollout_logp, rollout_row):
     slices = head_weight.T
-    stream, mine, other = prepare(hidden, norm_gain, token_ids, slices)
+    stream, mine, other, rows = prepare(hidden, norm_gain, token_ids, rollout_logp, slices)
     partner = lax.ppermute(stream, "dp", shift(2, 1))
     own_toks = token_ring(stream, 1)
 
@@ -346,10 +355,8 @@
     heads += head_ring(jnp.stack([near, lax.ppermute(near, "core", shift(2, 1))]), 1)
     partner_toks = token_ring(partner, -1)
 
-    refs = jnp.broadcast_to(rollout_logp, (32, 1, 64))
-    refs = lax.all_to_all(refs, ("dp", "xh", "y", "core"), 0, 0, tiled=True)
+    refs = lax.all_to_all(rows, ("dp", "xh", "y", "core"), 0, 0, tiled=True)
     own_ref = lax.dynamic_index_in_dim(refs[:, 0], rollout_row[0], 0)
-    own_ref = jnp.pad(own_ref, ((0, 7), (0, 64)))
 
     send = head_stats(own_toks, partner_toks, heads, own_ref)
     got = lax.all_to_all(send, ("dp", "tensor"), 0, 0, tiled=True)

time: 181 us -> 180 us (level)
  no operation moved by 1% of the time
where the time goes in v2:
time: 180 us
  waiting for transfers between devices  85.1 us (47%)
  starting transfers between devices  51.8 us (29%)
  Pallas kernels  24.1 us (13%)
  blocking collectives  12.8 us (7%)
  between operations  2.14 us (1%)
  other arithmetic  1.91 us (1%)
    ppermute x6, waiting for transfers between devices, token_ring(): ahead = lax.ppermute(ahead, 'tensor', shift(8, -1))  22.8 us
    pallas_call x1, Pallas kernels, head_stats(): pl.pallas_call(head_kernel, out_shape=jax.ShapeDtypeStruct((16, 24, 128),...  19.1 us
    ppermute x2, waiting for transfers between devices, head_ring(): near = lax.ppermute(block, ('y', 'core'), two_way_y())  18.3 us
    ppermute x6, starting transfers between devices, token_ring(): ahead = lax.ppermute(ahead, 'tensor', shift(8, -1))  13 us
    all_to_all x1, blocking collectives, steps(): lax.all_to_all(parts, ('dp', 'xh', 'y', 'core'), 0, 0, tiled=True)  12.8 us
    ppermute x6, waiting for transfers between devices, token_ring(): back = lax.ppermute(back, 'tensor', shift(8, 1))  11.7 us
    ppermute x1, waiting for transfers between devices, steps(): near = lax.ppermute(other, ('dp', 'xh'), X_NEAR)  9.75 us
    ppermute x2, waiting for transfers between devices, token_ring(): return out + [lax.ppermute(far, 'tensor', shift(8, far_step))]  9.69 us
  transfers between devices with their start and end apart: 28, of which 14 were waited for; matrix products, arithmetic and copies ran while one was open for 1% of the time, Pallas kernels for 0%

profile of v2, /device:TPU:1, one launch (start us, length us, event | category | flops | bytes accessed | tf_op | source)
XLA Modules:
  0.0 179.6 jit_solution(12948779822252308039)
XLA Ops:
  0.6 3.3 %prepare.1 = (bf16[528,256]{1,0:T(8,128)(2,1)}, bf16[2008,128]{1,0:T(8,128)(2,1)}, bf16[2008,128]{1,0:T(8,128)(2,1)}, f32[32,1,64]{2,1,0:T(1,128)}) custom-call(bf16[512,256]{1,0:T(8,128)(2,1)} %hidden_ref.1, bf16[256]{0:T(256)(128)(2,1)} %gain_ref.1, s32[1,512]{1,0:T(1,128)} %ids_ref.1, f32[1,64]{1,0:T(1,128)} %logp_ref.1, bf16[4016,128]{1,0:T(8,128)(2,1)} %bitcast.13), custom_call_target="tpu_custom_call" | custom-call | tf_op jit(solution)/shard_map/prepare/pallas_call | solution.py:60
  3.9 3.4 %collective-permute-start.20 = (bf16[2008,128]{1,0:T(8,128)(2,1)}, bf16[2008,128]{1,0:T(8,128)(2,1)S(1)}, u32[]{:S(2)}, u32[]{:S(2)}) collective-permute-start(bf16[2008,128]{1,0:T(8,128)(2,1)} %get-tuple-element.12), channel_id=1, source_target_pairs={{128,64},{64,128},{192,0},{0,192},{129,65},{65,129},{193,1},{1,193... | collective-permute-start | bytes 1542152 | tf_op jit(solution)/shard_map/ppermute | solution.py:353
  8.3 9.7 %collective-permute-done.20 = bf16[2008,128]{1,0:T(8,128)(2,1)S(1)} collective-permute-done((bf16[2008,128]{1,0:T(8,128)(2,1)}, bf16[2008,128]{1,0:T(8,128)(2,1)S(1)}, u32[]{:S(2)}, u32[]{:S(2)}) %collective-permute-start.20) | collective-permute-done | bytes 514080 | tf_op jit(solution)/shard_map/ppermute | solution.py:353
  18.0 2.2 %collective-permute-start.21 = (bf16[2008,128]{1,0:T(8,128)(2,1)S(1)}, bf16[2008,128]{1,0:T(8,128)(2,1)S(1)}, u32[]{:S(2)}, u32[]{:S(2)}) collective-permute-start(bf16[2008,128]{1,0:T(8,128)(2,1)S(1)} %collective-permute-done.20), channel_id=1, source_target_pairs={{0,8},{8,0},{1,9},{9,1},{2,10},{10,2},{3,11},{11,3},{4,12},{12,4},... | collective-permute-start | bytes 1542152 | tf_op jit(solution)/shard_map/ppermute | solution.py:355
  21.3 3.0 %collective-permute-start.16 = (bf16[2,2008,128]{2,1,0:T(8,128)(2,1)S(1)}, bf16[2,2008,128]{2,1,0:T(8,128)(2,1)S(1)}, u32[]{:S(2)}, u32[]{:S(2)}) collective-permute-start(bf16[2,2008,128]{2,1,0:T(8,128)(2,1)S(1)} %pad_maximum_fusion.refs_16_), channel_id=1, source_target_pairs={{0,16},{16,32},{32,48},{48,0},{8,56},{24,8},{40,24},{56,40},{1,17}... | collective-permute-start | bytes 3084296 | tf_op jit(solution)/shard_map/ppermute | solution.py:339
  25.3 1.6 collective-permute-start
  26.9 8.9 %collective-permute-done.16.refs_17_ = bf16[2,2008,128]{2,1,0:T(8,128)(2,1)S(1)} collective-permute-done((bf16[2,2008,128]{2,1,0:T(8,128)(2,1)S(1)}, bf16[2,2008,128]{2,1,0:T(8,128)(2,1)S(1)}, u32[]{:S(2)}, u32[]{:S(2)}) %collective-permute-start.16) | collective-permute-done | bytes 1028128 | tf_op jit(solution)/shard_map/ppermute | solution.py:339
  35.9 1.6 collective-permute-start.18
  37.5 9.4 %collective-permute-done.22.refs_22_ = bf16[2,2008,128]{2,1,0:T(8,128)(2,1)S(1)} collective-permute-done((bf16[2,2008,128]{2,1,0:T(8,128)(2,1)S(1)}, bf16[2,2008,128]{2,1,0:T(8,128)(2,1)S(1)}, u32[]{:S(2)}, u32[]{:S(2)}) %collective-permute-start.22) | collective-permute-done | bytes 1028128 | tf_op jit(solution)/shard_map/ppermute | solution.py:339
  46.9 5.0 %collective-permute-start.24 = (bf16[2,2008,128]{2,1,0:T(8,128)(2,1)S(1)}, bf16[2,2008,128]{2,1,0:T(8,128)(2,1)}, u32[]{:S(2)}, u32[]{:S(2)}) collective-permute-start(bf16[2,2008,128]{2,1,0:T(8,128)(2,1)S(1)} %collective-permute-done.22.refs_22_), channel_id=1, source_target_pairs={{8,56},{24,8},{40,24},{56,40},{9,57},{25,9},{41,25},{57,41},{10,58... | collective-permute-start | bytes 3084296 | tf_op jit(solution)/shard_map/ppermute | solution.py:341
  51.9 5.7 %collective-permute-start.1 = (bf16[528,256]{1,0:T(8,128)(2,1)S(1)}, bf16[528,256]{1,0:T(8,128)(2,1)S(1)}, u32[]{:S(2)}, u32[]{:S(2)}) collective-permute-start(bf16[528,256]{1,0:T(8,128)(2,1)S(1)} %copy-done.5), channel_id=1, source_target_pairs={{0,7},{1,0},{2,1},{3,2},{4,3},{5,4},{6,5},{7,6},{8,15},{9,8},{10,9... | collective-permute-start | bytes 811016 | tf_op jit(solution)/shard_map/ppermute | solution.py:332
  59.0 4.8 %collective-permute-done.1.refs_2_ = bf16[528,256]{1,0:T(8,128)(2,1)S(1)} collective-permute-done((bf16[528,256]{1,0:T(8,128)(2,1)S(1)}, bf16[528,256]{1,0:T(8,128)(2,1)S(1)}, u32[]{:S(2)}, u32[]{:S(2)}) %collective-permute-start.1) | collective-permute-done | bytes 270368 | tf_op jit(solution)/shard_map/ppermute | solution.py:332
  63.9 4.3 %collective-permute-done.9.refs_10_ = bf16[528,256]{1,0:T(8,128)(2,1)S(1)} collective-permute-done((bf16[528,256]{1,0:T(8,128)(2,1)S(1)}, bf16[528,256]{1,0:T(8,128)(2,1)S(1)}, u32[]{:S(2)}, u32[]{:S(2)}) %collective-permute-start.9) | collective-permute-done | bytes 270368 | tf_op jit(solution)/shard_map/ppermute | solution.py:332
  68.2 3.1 %collective-permute-start.3 = (bf16[528,256]{1,0:T(8,128)(2,1)S(1)}, bf16[528,256]{1,0:T(8,128)(2,1)S(1)}, u32[]{:S(2)}, u32[]{:S(2)}) collective-permute-start(bf16[528,256]{1,0:T(8,128)(2,1)S(1)} %collective-permute-done.1.refs_2_), channel_id=1, source_target_pairs={{0,7},{1,0},{2,1},{3,2},{4,3},{5,4},{6,5},{7,6},{8,15},{9,8},{10,9... | collective-permute-start | bytes 811016 | tf_op jit(solution)/shard_map/ppermute | solution.py:332
  71.4 1.2 collective-permute-done.2.refs_3_
  72.8 4.8 %collective-permute-done.3.refs_4_ = bf16[528,256]{1,0:T(8,128)(2,1)S(1)} collective-permute-done((bf16[528,256]{1,0:T(8,128)(2,1)S(1)}, bf16[528,256]{1,0:T(8,128)(2,1)S(1)}, u32[]{:S(2)}, u32[]{:S(2)}) %collective-permute-start.3) | collective-permute-done | bytes 270368 | tf_op jit(solution)/shard_map/ppermute | solution.py:332
  77.6 5.5 %collective-permute-done.11.refs_12_ = bf16[528,256]{1,0:T(8,128)(2,1)S(1)} collective-permute-done((bf16[528,256]{1,0:T(8,128)(2,1)S(1)}, bf16[528,256]{1,0:T(8,128)(2,1)S(1)}, u32[]{:S(2)}, u32[]{:S(2)}) %collective-permute-start.11) | collective-permute-done | bytes 270368 | tf_op jit(solution)/shard_map/ppermute | solution.py:332
  83.1 3.1 %collective-permute-start.5 = (bf16[528,256]{1,0:T(8,128)(2,1)S(1)}, bf16[528,256]{1,0:T(8,128)(2,1)S(1)}, u32[]{:S(2)}, u32[]{:S(2)}) collective-permute-start(bf16[528,256]{1,0:T(8,128)(2,1)S(1)} %collective-permute-done.3.refs_4_), channel_id=1, source_target_pairs={{0,7},{1,0},{2,1},{3,2},{4,3},{5,4},{6,5},{7,6},{8,15},{9,8},{10,9... | collective-permute-start | bytes 811016 | tf_op jit(solution)/shard_map/ppermute | solution.py:332
  86.5 1.5 collective-permute-done.4.refs_5_
  88.4 3.3 %collective-permute-done.5.refs_6_ = bf16[528,256]{1,0:T(8,128)(2,1)S(1)} collective-permute-done((bf16[528,256]{1,0:T(8,128)(2,1)S(1)}, bf16[528,256]{1,0:T(8,128)(2,1)S(1)}, u32[]{:S(2)}, u32[]{:S(2)}) %collective-permute-start.5) | collective-permute-done | bytes 270368 | tf_op jit(solution)/shard_map/ppermute | solution.py:332
  91.7 2.1 %collective-permute-start.23 = (bf16[2,2008,128]{2,1,0:T(8,128)(2,1)S(1)}, bf16[2,2008,128]{2,1,0:T(8,128)(2,1)}, u32[]{:S(2)}, u32[]{:S(2)}) collective-permute-start(bf16[2,2008,128]{2,1,0:T(8,128)(2,1)S(1)} %collective-permute-done.22.refs_22_), channel_id=1, source_target_pairs={{0,8},{8,0},{1,9},{9,1},{2,10},{10,2},{3,11},{11,3},{4,12},{12,4},... | collective-permute-start | bytes 3084296 | tf_op jit(solution)/shard_map/ppermute | solution.py:342
  93.8 1.3 collective-permute-start.19
  95.1 5.0 %collective-permute-start.25 = (bf16[2,2008,128]{2,1,0:T(8,128)(2,1)}, bf16[2,2008,128]{2,1,0:T(8,128)(2,1)}, u32[]{:S(2)}, u32[]{:S(2)}) collective-permute-start(bf16[2,2008,128]{2,1,0:T(8,128)(2,1)} %collective-permute-done.24.refs_24_), channel_id=1, source_target_pairs={{8,0},{9,1},{10,2},{11,3},{12,4},{13,5},{14,6},{15,7},{24,16},{25,... | collective-permute-start | bytes 3084296 | tf_op jit(solution)/shard_map/ppermute | solution.py:343
  100.2 9.0 %collective-permute-done.12.refs_13_ = bf16[528,256]{1,0:T(8,128)(2,1)S(1)} collective-permute-done((bf16[528,256]{1,0:T(8,128)(2,1)S(1)}, bf16[528,256]{1,0:T(8,128)(2,1)S(1)}, u32[]{:S(2)}, u32[]{:S(2)}) %collective-permute-start.12) | collective-permute-done | bytes 270368 | tf_op jit(solution)/shard_map/ppermute | solution.py:331
  109.2 9.7 %collective-permute-done.6.refs_7_ = bf16[528,256]{1,0:T(8,128)(2,1)S(1)} collective-permute-done((bf16[528,256]{1,0:T(8,128)(2,1)S(1)}, bf16[528,256]{1,0:T(8,128)(2,1)S(1)}, u32[]{:S(2)}, u32[]{:S(2)}) %collective-permute-start.6) | collective-permute-done | bytes 270368 | tf_op jit(solution)/shard_map/ppermute | solution.py:335
  119.6 6.7 %all-to-all-start = ((f32[32,1,64]{2,1,0:T(1,128)}), f32[32,1,64]{2,1,0:T(1,128)S(1)}, u32[]{:S(2)}, u32[]{:S(2)}) async-start(f32[32,1,64]{2,1,0:T(1,128)} %get-tuple-element.13), calls=%async_computation | async-start | bytes 32768 | tf_op jit(solution)/shard_map/all_to_all | solution.py:358
  127.0 6.1 %all-to-all-done = f32[32,1,64]{2,1,0:T(1,128)S(1)} async-done(((f32[32,1,64]{2,1,0:T(1,128)}), f32[32,1,64]{2,1,0:T(1,128)S(1)}, u32[]{:S(2)}, u32[]{:S(2)}) %all-to-all-start) | async-done | bytes 8224 | tf_op jit(solution)/shard_map/all_to_all | solution.py:358
  133.7 19.1 %head_stats.1 = f32[16,24,128]{2,1,0:T(8,128)} custom-call(bf16[528,256]{1,0:T(8,128)(2,1)} %get-tuple-element.10.refs_0_, bf16[528,256]{1,0:T(8,128)(2,1)} %copy-done.7, bf16[528,256]{1,0:T(8,128)(2,1)} %copy-done.8, bf16[528,256]{1,0:T(8,128)(2,1)} %copy-done.11, bf16[528,256]{1,0:T(8,128)(2,1)} %copy-done.12, bf16[528,256]{1,0:T(8,128)(2,1)} %copy-done.15, ...), custom_call_target="tpu_custom_call" | custom-call | flops 8422162432 | bytes 13631488 | tf_op jit(solution)/shard_map/head_stats/pallas_call | solution.py:229
  152.8 3.5 %all-to-all-start.1 = ((f32[16,24,128]{2,1,0:T(8,128)}), f32[16,24,128]{2,1,0:T(8,128)S(1)}, u32[]{:S(2)}, u32[]{:S(2)}) async-start(f32[16,24,128]{2,1,0:T(8,128)} %head_stats.1), calls=%async_computation.1 | async-start | bytes 393216 | tf_op jit(solution)/shard_map/all_to_all | solution.py:362
  156.9 6.8 %all-to-all-done.1.got_ref = f32[16,24,128]{2,1,0:T(8,128)S(1)} async-done(((f32[16,24,128]{2,1,0:T(8,128)}), f32[16,24,128]{2,1,0:T(8,128)S(1)}, u32[]{:S(2)}, u32[]{:S(2)}) %all-to-all-start.1) | async-done | bytes 196640 | tf_op jit(solution)/shard_map/all_to_all | solution.py:362
  164.4 1.7 combine.1
  166.1 12.8 %all_to_all.15 = f32[32,1,128]{2,1,0:T(1,128)S(1)} all-to-all(f32[32,1,128]{2,1,0:T(1,128)} %get-tuple-element.16), channel_id=1, replica_groups=mesh['dp'=2,'xh'=2,'y'=4,'core'=2,'tensor'=8] {'dp','xh','y','core'}, dimensions={0} | all-to-all | bytes 32768 | tf_op jit(solution)/shard_map/all_to_all | solution.py:364
  (71 shorter events, 8.2 us)
Async XLA Ops:
  3.9 14.1 %collective-permute-start.20 = (bf16[2008,128]{1,0:T(8,128)(2,1)}, bf16[2008,128]{1,0:T(8,128)(2,1)S(1)}, u32[]{:S(2)}, u32[]{:S(2)}) collective-permute-start(bf16[2008,128]{1,0:T(8,128)(2,1)} %get-tuple-element.12), channel_id=1, source_target_pairs={{128,64},{64,128},{192,0},{0,192},{129,65},{65,129},{193,1},{1,193... | collective-permute-start | bytes 1542152 | tf_op jit(solution)/shard_map/ppermute | solution.py:353
  7.3 12.9 %collective-permute-start.15 = (bf16[2008,128]{1,0:T(8,128)(2,1)}, bf16[2008,128]{1,0:T(8,128)(2,1)S(1)}, u32[]{:S(2)}, u32[]{:S(2)}) collective-permute-start(bf16[2008,128]{1,0:T(8,128)(2,1)} %get-tuple-element.11), channel_id=1, source_target_pairs={{0,8},{8,0},{1,9},{9,1},{2,10},{10,2},{3,11},{11,3},{4,12},{12,4},... | collective-permute-start | bytes 1542152 | tf_op jit(solution)/shard_map/ppermute | solution.py:354
  18.0 6.3 %collective-permute-start.21 = (bf16[2008,128]{1,0:T(8,128)(2,1)S(1)}, bf16[2008,128]{1,0:T(8,128)(2,1)S(1)}, u32[]{:S(2)}, u32[]{:S(2)}) collective-permute-start(bf16[2008,128]{1,0:T(8,128)(2,1)S(1)} %collective-permute-done.20), channel_id=1, source_target_pairs={{0,8},{8,0},{1,9},{9,1},{2,10},{10,2},{3,11},{11,3},{4,12},{12,4},... | collective-permute-start | bytes 1542152 | tf_op jit(solution)/shard_map/ppermute | solution.py:355
  21.3 14.5 %collective-permute-start.16 = (bf16[2,2008,128]{2,1,0:T(8,128)(2,1)S(1)}, bf16[2,2008,128]{2,1,0:T(8,128)(2,1)S(1)}, u32[]{:S(2)}, u32[]{:S(2)}) collective-permute-start(bf16[2,2008,128]{2,1,0:T(8,128)(2,1)S(1)} %pad_maximum_fusion.refs_16_), channel_id=1, source_target_pairs={{0,16},{16,32},{32,48},{48,0},{8,56},{24,8},{40,24},{56,40},{1,17}... | collective-permute-start | bytes 3084296 | tf_op jit(solution)/shard_map/ppermute | solution.py:339
  24.5 109.2 %copy-start.1 = (bf16[2,2008,128]{2,1,0:T(8,128)(2,1)}, bf16[2,2008,128]{2,1,0:T(8,128)(2,1)S(1)}, u32[]{:S(2)}) copy-start(bf16[2,2008,128]{2,1,0:T(8,128)(2,1)S(1)} %pad_maximum_fusion.1.refs_21_) | copy-start | bytes 3084292
  24.5 22.4 %collective-permute-start.22 = (bf16[2,2008,128]{2,1,0:T(8,128)(2,1)S(1)}, bf16[2,2008,128]{2,1,0:T(8,128)(2,1)S(1)}, u32[]{:S(2)}, u32[]{:S(2)}) collective-permute-start(bf16[2,2008,128]{2,1,0:T(8,128)(2,1)S(1)} %pad_maximum_fusion.1.refs_21_), channel_id=1, source_target_pairs={{0,16},{16,32},{32,48},{48,0},{8,56},{24,8},{40,24},{56,40},{1,17}... | collective-permute-start | bytes 3084296 | tf_op jit(solution)/shard_map/ppermute | solution.py:339
  25.3 32.3 %collective-permute-start.7 = (bf16[528,256]{1,0:T(8,128)(2,1)S(1)}, bf16[528,256]{1,0:T(8,128)(2,1)S(1)}, u32[]{:S(2)}, u32[]{:S(2)}) collective-permute-start(bf16[528,256]{1,0:T(8,128)(2,1)S(1)} %copy-done.5), channel_id=1, source_target_pairs={{0,128},{128,0},{1,129},{129,1},{2,130},{130,2},{3,131},{131,3},{4... | collective-permute-start | bytes 811016 | tf_op jit(solution)/shard_map/ppermute | solution.py:350
  25.3 33.0 %collective-permute-start = (bf16[528,256]{1,0:T(8,128)(2,1)S(1)}, bf16[528,256]{1,0:T(8,128)(2,1)S(1)}, u32[]{:S(2)}, u32[]{:S(2)}) collective-permute-start(bf16[528,256]{1,0:T(8,128)(2,1)S(1)} %copy-done.5), channel_id=1, source_target_pairs={{0,1},{1,2},{2,3},{3,4},{4,5},{5,6},{6,7},{7,0},{8,9},{9,10},{10,1... | collective-permute-start | bytes 811016 | tf_op jit(solution)/shard_map/ppermute | solution.py:331
  35.9 97.8 %copy-start.3 = (bf16[2,2008,128]{2,1,0:T(8,128)(2,1)}, bf16[2,2008,128]{2,1,0:T(8,128)(2,1)S(1)}, u32[]{:S(2)}) copy-start(bf16[2,2008,128]{2,1,0:T(8,128)(2,1)S(1)} %collective-permute-done.16.refs_17_) | copy-start | bytes 3084292
  35.9 57.9 %collective-permute-start.18 = (bf16[2,2008,128]{2,1,0:T(8,128)(2,1)S(1)}, bf16[2,2008,128]{2,1,0:T(8,128)(2,1)}, u32[]{:S(2)}, u32[]{:S(2)}) collective-permute-start(bf16[2,2008,128]{2,1,0:T(8,128)(2,1)S(1)} %collective-permute-done.16.refs_17_), channel_id=1, source_target_pairs={{0,16},{16,32},{32,48},{48,0},{1,17},{17,33},{33,49},{49,1},{2,18}... | collective-permute-start | bytes 3084296 | tf_op jit(solution)/shard_map/ppermute | solution.py:341
  46.9 86.8 %copy-start.4 = (bf16[2,2008,128]{2,1,0:T(8,128)(2,1)}, bf16[2,2008,128]{2,1,0:T(8,128)(2,1)S(1)}, u32[]{:S(2)}) copy-start(bf16[2,2008,128]{2,1,0:T(8,128)(2,1)S(1)} %collective-permute-done.22.refs_22_) | copy-start | bytes 3084292
  46.9 48.2 %collective-permute-start.24 = (bf16[2,2008,128]{2,1,0:T(8,128)(2,1)S(1)}, bf16[2,2008,128]{2,1,0:T(8,128)(2,1)}, u32[]{:S(2)}, u32[]{:S(2)}) collective-permute-start(bf16[2,2008,128]{2,1,0:T(8,128)(2,1)S(1)} %collective-permute-done.22.refs_22_), channel_id=1, source_target_pairs={{8,56},{24,8},{40,24},{56,40},{9,57},{25,9},{41,25},{57,41},{10,58... | collective-permute-start | bytes 3084296 | tf_op jit(solution)/shard_map/ppermute | solution.py:341
  51.9 11.9 %collective-permute-start.1 = (bf16[528,256]{1,0:T(8,128)(2,1)S(1)}, bf16[528,256]{1,0:T(8,128)(2,1)S(1)}, u32[]{:S(2)}, u32[]{:S(2)}) collective-permute-start(bf16[528,256]{1,0:T(8,128)(2,1)S(1)} %copy-done.5), channel_id=1, source_target_pairs={{0,7},{1,0},{2,1},{3,2},{4,3},{5,4},{6,5},{7,6},{8,15},{9,8},{10,9... | collective-permute-start | bytes 811016 | tf_op jit(solution)/shard_map/ppermute | solution.py:332
  57.6 10.6 %collective-permute-start.9 = (bf16[528,256]{1,0:T(8,128)(2,1)S(1)}, bf16[528,256]{1,0:T(8,128)(2,1)S(1)}, u32[]{:S(2)}, u32[]{:S(2)}) collective-permute-start(bf16[528,256]{1,0:T(8,128)(2,1)S(1)} %collective-permute-done.7.refs_8_), channel_id=1, source_target_pairs={{0,7},{1,0},{2,1},{3,2},{4,3},{5,4},{6,5},{7,6},{8,15},{9,8},{10,9... | collective-permute-start | bytes 811016 | tf_op jit(solution)/shard_map/ppermute | solution.py:332
  58.3 13.0 %collective-permute-start.8 = (bf16[528,256]{1,0:T(8,128)(2,1)S(1)}, bf16[528,256]{1,0:T(8,128)(2,1)S(1)}, u32[]{:S(2)}, u32[]{:S(2)}) collective-permute-start(bf16[528,256]{1,0:T(8,128)(2,1)S(1)} %collective-permute-done.7.refs_8_), channel_id=1, source_target_pairs={{0,1},{1,2},{2,3},{3,4},{4,5},{5,6},{6,7},{7,0},{8,9},{9,10},{10,1... | collective-permute-start | bytes 811016 | tf_op jit(solution)/shard_map/ppermute | solution.py:331
  63.9 8.8 %collective-permute-start.2 = (bf16[528,256]{1,0:T(8,128)(2,1)S(1)}, bf16[528,256]{1,0:T(8,128)(2,1)S(1)}, u32[]{:S(2)}, u32[]{:S(2)}) collective-permute-start(bf16[528,256]{1,0:T(8,128)(2,1)S(1)} %collective-permute-done.refs_1_), channel_id=1, source_target_pairs={{0,1},{1,2},{2,3},{3,4},{4,5},{5,6},{6,7},{7,0},{8,9},{9,10},{10,1... | collective-permute-start | bytes 811016 | tf_op jit(solution)/shard_map/ppermute | solution.py:331
  68.2 9.4 %collective-permute-start.3 = (bf16[528,256]{1,0:T(8,128)(2,1)S(1)}, bf16[528,256]{1,0:T(8,128)(2,1)S(1)}, u32[]{:S(2)}, u32[]{:S(2)}) collective-permute-start(bf16[528,256]{1,0:T(8,128)(2,1)S(1)} %collective-permute-done.1.refs_2_), channel_id=1, source_target_pairs={{0,7},{1,0},{2,1},{3,2},{4,3},{5,4},{6,5},{7,6},{8,15},{9,8},{10,9... | collective-permute-start | bytes 811016 | tf_op jit(solution)/shard_map/ppermute | solution.py:332
  71.3 11.8 %collective-permute-start.11 = (bf16[528,256]{1,0:T(8,128)(2,1)S(1)}, bf16[528,256]{1,0:T(8,128)(2,1)S(1)}, u32[]{:S(2)}, u32[]{:S(2)}) collective-permute-start(bf16[528,256]{1,0:T(8,128)(2,1)S(1)} %collective-permute-done.9.refs_10_), channel_id=1, source_target_pairs={{0,7},{1,0},{2,1},{3,2},{4,3},{5,4},{6,5},{7,6},{8,15},{9,8},{10,9... | collective-permute-start | bytes 811016 | tf_op jit(solution)/shard_map/ppermute | solution.py:332
  72.6 61.0 %copy-start.11 = (bf16[528,256]{1,0:T(8,128)(2,1)}, bf16[528,256]{1,0:T(8,128)(2,1)S(1)}, u32[]{:S(2)}) copy-start(bf16[528,256]{1,0:T(8,128)(2,1)S(1)} %collective-permute-done.2.refs_3_) | copy-start | bytes 811012
  72.6 13.6 %collective-permute-start.10 = (bf16[528,256]{1,0:T(8,128)(2,1)S(1)}, bf16[528,256]{1,0:T(8,128)(2,1)S(1)}, u32[]{:S(2)}, u32[]{:S(2)}) collective-permute-start(bf16[528,256]{1,0:T(8,128)(2,1)S(1)} %collective-permute-done.8.refs_9_), channel_id=1, source_target_pairs={{0,1},{1,2},{2,3},{3,4},{4,5},{5,6},{6,7},{7,0},{8,9},{9,10},{10,1... | collective-permute-start | bytes 811016 | tf_op jit(solution)/shard_map/ppermute | solution.py:331
  77.6 10.4 %collective-permute-start.4 = (bf16[528,256]{1,0:T(8,128)(2,1)S(1)}, bf16[528,256]{1,0:T(8,128)(2,1)S(1)}, u32[]{:S(2)}, u32[]{:S(2)}) collective-permute-start(bf16[528,256]{1,0:T(8,128)(2,1)S(1)} %collective-permute-done.2.refs_3_), channel_id=1, source_target_pairs={{0,1},{1,2},{2,3},{3,4},{4,5},{5,6},{6,7},{7,0},{8,9},{9,10},{10,1... | collective-permute-start | bytes 811016 | tf_op jit(solution)/shard_map/ppermute | solution.py:331
  83.1 8.6 %collective-permute-start.5 = (bf16[528,256]{1,0:T(8,128)(2,1)S(1)}, bf16[528,256]{1,0:T(8,128)(2,1)S(1)}, u32[]{:S(2)}, u32[]{:S(2)}) collective-permute-start(bf16[528,256]{1,0:T(8,128)(2,1)S(1)} %collective-permute-done.3.refs_4_), channel_id=1, source_target_pairs={{0,7},{1,0},{2,1},{3,2},{4,3},{5,4},{6,5},{7,6},{8,15},{9,8},{10,9... | collective-permute-start | bytes 811016 | tf_op jit(solution)/shard_map/ppermute | solution.py:332
  86.2 13.8 %collective-permute-start.13 = (bf16[528,256]{1,0:T(8,128)(2,1)S(1)}, bf16[528,256]{1,0:T(8,128)(2,1)}, u32[]{:S(2)}, u32[]{:S(2)}) collective-permute-start(bf16[528,256]{1,0:T(8,128)(2,1)S(1)} %collective-permute-done.11.refs_12_), channel_id=1, source_target_pairs={{0,7},{1,0},{2,1},{3,2},{4,3},{5,4},{6,5},{7,6},{8,15},{9,8},{10,9... | collective-permute-start | bytes 811016 | tf_op jit(solution)/shard_map/ppermute | solution.py:332
  88.0 45.6 %collective-permute-start.17 = (bf16[2,2008,128]{2,1,0:T(8,128)(2,1)S(1)}, bf16[2,2008,128]{2,1,0:T(8,128)(2,1)}, u32[]{:S(2)}, u32[]{:S(2)}) collective-permute-start(bf16[2,2008,128]{2,1,0:T(8,128)(2,1)S(1)} %collective-permute-done.16.refs_17_), channel_id=1, source_target_pairs={{0,8},{8,0},{1,9},{9,1},{2,10},{10,2},{3,11},{11,3},{4,12},{12,4},... | collective-permute-start | bytes 3084296 | tf_op jit(solution)/shard_map/ppermute | solution.py:342
  91.7 41.9 %collective-permute-start.23 = (bf16[2,2008,128]{2,1,0:T(8,128)(2,1)S(1)}, bf16[2,2008,128]{2,1,0:T(8,128)(2,1)}, u32[]{:S(2)}, u32[]{:S(2)}) collective-permute-start(bf16[2,2008,128]{2,1,0:T(8,128)(2,1)S(1)} %collective-permute-done.22.refs_22_), channel_id=1, source_target_pairs={{0,8},{8,0},{1,9},{9,1},{2,10},{10,2},{3,11},{11,3},{4,12},{12,4},... | collective-permute-start | bytes 3084296 | tf_op jit(solution)/shard_map/ppermute | solution.py:342
  93.8 39.8 %collective-permute-start.19 = (bf16[2,2008,128]{2,1,0:T(8,128)(2,1)}, bf16[2,2008,128]{2,1,0:T(8,128)(2,1)}, u32[]{:S(2)}, u32[]{:S(2)}) collective-permute-start(bf16[2,2008,128]{2,1,0:T(8,128)(2,1)} %collective-permute-done.18.refs_19_), channel_id=1, source_target_pairs={{0,8},{1,9},{2,10},{3,11},{4,12},{5,13},{6,14},{7,15},{16,24},{17,... | collective-permute-start | bytes 3084296 | tf_op jit(solution)/shard_map/ppermute | solution.py:343
  95.1 38.5 %collective-permute-start.25 = (bf16[2,2008,128]{2,1,0:T(8,128)(2,1)}, bf16[2,2008,128]{2,1,0:T(8,128)(2,1)}, u32[]{:S(2)}, u32[]{:S(2)}) collective-permute-start(bf16[2,2008,128]{2,1,0:T(8,128)(2,1)} %collective-permute-done.24.refs_24_), channel_id=1, source_target_pairs={{8,0},{9,1},{10,2},{11,3},{12,4},{13,5},{14,6},{15,7},{24,16},{25,... | collective-permute-start | bytes 3084296 | tf_op jit(solution)/shard_map/ppermute | solution.py:343
  100.1 9.1 %collective-permute-start.12 = (bf16[528,256]{1,0:T(8,128)(2,1)S(1)}, bf16[528,256]{1,0:T(8,128)(2,1)S(1)}, u32[]{:S(2)}, u32[]{:S(2)}) collective-permute-start(bf16[528,256]{1,0:T(8,128)(2,1)S(1)} %collective-permute-done.10.refs_11_), channel_id=1, source_target_pairs={{0,1},{1,2},{2,3},{3,4},{4,5},{5,6},{6,7},{7,0},{8,9},{9,10},{10,1... | collective-permute-start | bytes 811016 | tf_op jit(solution)/shard_map/ppermute | solution.py:331
  109.2 9.7 %collective-permute-start.6 = (bf16[528,256]{1,0:T(8,128)(2,1)S(1)}, bf16[528,256]{1,0:T(8,128)(2,1)S(1)}, u32[]{:S(2)}, u32[]{:S(2)}) collective-permute-start(bf16[528,256]{1,0:T(8,128)(2,1)S(1)} %collective-permute-done.4.refs_5_), channel_id=1, source_target_pairs={{0,1},{1,2},{2,3},{3,4},{4,5},{5,6},{6,7},{7,0},{8,9},{9,10},{10,1... | collective-permute-start | bytes 811016 | tf_op jit(solution)/shard_map/ppermute | solution.py:335
  118.9 14.7 %collective-permute-start.14 = (bf16[528,256]{1,0:T(8,128)(2,1)}, bf16[528,256]{1,0:T(8,128)(2,1)}, u32[]{:S(2)}, u32[]{:S(2)}) collective-permute-start(bf16[528,256]{1,0:T(8,128)(2,1)} %collective-permute-done.13.refs_14_), channel_id=1, source_target_pairs={{0,7},{1,0},{2,1},{3,2},{4,3},{5,4},{6,5},{7,6},{8,15},{9,8},{10,9... | collective-permute-start | bytes 811016 | tf_op jit(solution)/shard_map/ppermute | solution.py:335
  119.6 13.5 %all-to-all-start = ((f32[32,1,64]{2,1,0:T(1,128)}), f32[32,1,64]{2,1,0:T(1,128)S(1)}, u32[]{:S(2)}, u32[]{:S(2)}) async-start(f32[32,1,64]{2,1,0:T(1,128)} %get-tuple-element.13), calls=%async_computation | async-start | bytes 32768 | tf_op jit(solution)/shard_map/all_to_all | solution.py:358
  152.8 11.0 %all-to-all-start.1 = ((f32[16,24,128]{2,1,0:T(8,128)}), f32[16,24,128]{2,1,0:T(8,128)S(1)}, u32[]{:S(2)}, u32[]{:S(2)}) async-start(f32[16,24,128]{2,1,0:T(8,128)} %head_stats.1), calls=%async_computation.1 | async-start | bytes 393216 | tf_op jit(solution)/shard_map/all_to_all | solution.py:362
  (15 other events, 359.6 us)
